TPU v7x, 32 devices: a whole 2x2x4 slice. The times are simulated.
32 devices in a mesh: gx: 4 (over y, x), gy: 8 (over z, core).
Axes of the slice: x: 2, y: 2, z: 4, core: 2. Of those that a mesh axis runs over, the one named last changes fastest.
Arguments:
- volume: float32 [128, 512, 256], P('gx', 'gy'), may hold values from -18 to 18, as said below
Outputs:
- denoised: float32 [128, 512, 256], P('gx', 'gy')
Inputs may be any that keep to these rules, and one draw needn't show every extreme that they name: `volume`: real values.
All inputs are finite; a program needn't handle non-finite values.
Results may differ from a plain program's by a relative error of at most 0.00002.
Values sent between devices are 32-bit elements; how exact they have to be, the bound alone decides.
A program may use at most 128 MiB of HBM per device.

v0:
```python
import functools
import math

import jax
import jax.numpy as jnp
import numpy as np
from jax import lax
from jax.experimental import pallas as pl
from jax.experimental.pallas import tpu as pltpu
from jax.sharding import PartitionSpec as P

ROOT3 = math.sqrt(3.0)
NEAR = math.sqrt(3.0) / 4.0
FAR = (math.sqrt(3.0) - 2.0) / 4.0
LOW = (math.sqrt(3.0) - 1.0) / math.sqrt(2.0)
HIGH = (math.sqrt(3.0) + 1.0) / math.sqrt(2.0)
LANES = 128
PAD = 8


def forward_matrix(size):
    lines = np.eye(size)
    even, odd = lines[:, 0::2], lines[:, 1::2]
    smooth = even + ROOT3 * odd
    detail = odd - NEAR * smooth - FAR * np.roll(smooth, 1, 1)
    smooth = smooth - np.roll(detail, -1, 1)
    return np.concatenate([LOW * smooth, HIGH * detail], 1)


def inverse_matrix(size):
    lines = np.eye(size)
    smooth, detail = lines[:, : size // 2] / LOW, lines[:, size // 2 :] / HIGH
    first = smooth + np.roll(detail, -1, 1)
    odd = detail + NEAR * first + FAR * np.roll(first, 1, 1)
    even = first - ROOT3 * odd
    return np.stack([even, odd], 2).reshape(size, size)


def halves(matrix, size):
    full = np.zeros((size, size))
    full[: matrix.shape[0], : matrix.shape[1]] = matrix
    high = full.astype(jnp.bfloat16)
    low = (full - high.astype(np.float64)).astype(jnp.bfloat16)
    return np.stack([high, low])


def times(values, w_ref):
    high = values.astype(jnp.bfloat16)
    low = (values - high.astype(jnp.float32)).astype(jnp.bfloat16)
    dot = functools.partial(jnp.dot, preferred_element_type=jnp.float32)
    return dot(high, w_ref[0]) + (dot(low, w_ref[0]) + dot(high, w_ref[1]))


def shrink(values, noise):
    return values - jnp.clip(values, -noise, noise)


def sums(even, odd):
    smooth = even + ROOT3 * odd
    return smooth, odd - NEAR * smooth


def undo(detail, first, before):
    odd = detail + NEAR * first + FAR * before
    return first - ROOT3 * odd, odd


def weave(even, odd):
    both = jnp.stack([even, odd], axis=1)
    return both.reshape((2 * even.shape[0],) + even.shape[1:])


def forward_rows(even, odd):
    axis = even.ndim - 2
    smooth, part = sums(even, odd)
    detail = part - FAR * pltpu.roll(smooth, 1, axis)
    return HIGH * detail, LOW * (smooth - pltpu.roll(detail, even.shape[axis] - 1, axis))


def kernel(shape, count_all, nx, ny, vol, g1, g2, g3, g4, g5, g6, o1, v1,
           w1, w2, w3, v2, v3,
           e1, hx1, sx1, hy1, sy1, hc1, sc1, xd1, xs1, s1s, s1d, d1s, d1d,
           e2, ht2, st2, xd2, xs2, ss, sd, ds, dd, ep3, t3d, t3s, r2, r1,
           p1s, p1d, part, total, send, recv, lsem, wsem):
    cx, cy, cz = shape
    hx, hy, qx, qy = cx // 2, cy // 2, cx // 4, cy // 4
    ix, iy = lax.axis_index("gx"), lax.axis_index("gy")

    def device(dx, dy):
        return (lax.rem(ix + dx + nx, nx), lax.rem(iy + dy + ny, ny))

    loads = [
        pltpu.make_async_copy(
            vol.at[:, :, pl.ds(h * LANES, LANES)],
            e1.at[:, h, pl.ds(PAD, cy), :], lsem.at[h])
        for h in range(2)
    ]
    weights = [
        pltpu.make_async_copy(src, dst, wsem.at[i])
        for i, (src, dst) in enumerate(
            zip((g1, g2, g3, g4, g5, g6), (w1, w2, w3, v1, v2, v3)))
    ]
    for c in loads + weights:
        c.start()

    greet = [(dx, dy) for dx in (-1, 0, 1) for dy in (-1, 0, 1) if dx or dy]
    greet += [(dx, 0) for dx in range(2, nx - 1)] + [(0, dy) for dy in range(2, ny - 1)]
    barrier = pltpu.get_barrier_semaphore()
    for d in greet:
        pl.semaphore_signal(barrier, inc=1, device_id=device(*d),
                            device_id_type=pl.DeviceIdType.MESH)

    slot = [0]
    started = []

    def post(src, dst, dx, dy):
        n = slot[0]
        slot[0] += 1
        c = pltpu.make_async_remote_copy(
            src_ref=src, dst_ref=dst, send_sem=send.at[n], recv_sem=recv.at[n],
            device_id=device(dx, dy), device_id_type=pl.DeviceIdType.MESH)
        c.start()
        started.append(c)
        return c

    for c in loads:
        c.wait()

    top = PAD + cy
    sx1[1] = sums(e1[0, :, PAD:top], e1[1, :, PAD:top])[1]
    sy1[1] = sums(e1[:, :, PAD : PAD + 1], e1[:, :, PAD + 1 : PAD + 2])[1]
    sx1[0] = sums(e1[cx - 2, :, PAD:top], e1[cx - 1, :, PAD:top])[0]
    sy1[0] = sums(e1[:, :, top - 2 : top - 1], e1[:, :, top - 1 : top])[0]
    for x in range(2):
        sc1[x, 1] = sums(sx1[x, :, 0:1], sx1[x, :, 1:2])[1]
        sc1[x, 0] = sums(sx1[x, :, cy - 2 : cy - 1], sx1[x, :, cy - 1 : cy])[0]
    pl.semaphore_wait(barrier, len(greet))
    step = (1, -1)
    post_x = lambda x: post(sx1.at[x], hx1.at[x, :, pl.ds(PAD, cy), :], step[x], 0)
    post_y = lambda y: post(sy1.at[y], hy1.at[y], 0, step[y])
    post_c = lambda x, y: post(sc1.at[x, y], hc1.at[x, y], step[x], step[y])
    now1 = [post_c(1, 1), post_x(1), post_y(1)]
    later1 = [post_c(0, 1), post_c(1, 0), post_c(0, 0), post_x(0), post_y(0)]

    def place(ref, rows, side):
        if side == 0:
            ref[..., PAD - 2 : PAD - 1, :] = rows
            ref[..., PAD - 1 : PAD, :] = jnp.zeros_like(rows)
        else:
            ref[..., top : top + 1, :] = -ROOT3 * rows
            ref[..., top + 1 : top + 2, :] = rows

    def pair1(n, rows=slice(None)):
        return sums(e1[2 * n, :, rows], e1[2 * n + 1, :, rows])

    def lift1(rows):
        def step(n, carry):
            _, part_n = pair1(n, rows)
            before, _ = pair1(n - 1, rows)
            detail = part_n - FAR * before
            xd1[n, :, rows] = HIGH * detail
            xs1[n, :, rows] = LOW * (before - detail)
            return carry

        lax.fori_loop(1, hx, step, 0)

    def coarse1(n, first, count):
        for h in range(2):
            load = lambda start: xs1[n, h, pl.ds(start + 2 * first, count, stride=2), :]
            s0, _ = sums(load(PAD), load(PAD + 1))
            _, tp = sums(load(PAD + 2), load(PAD + 3))
            s1s[n, h, PAD + first : PAD + first + count] = LOW * (s0 - (tp - FAR * s0))

    def coarse1_inner(n, carry):
        coarse1(n, 0, hy)
        return carry

    def coarse1_top(n, carry):
        coarse1(n, hy - 1, 1)
        return carry

    lift1(slice(PAD, top))
    lax.fori_loop(1, hx, coarse1_inner, 0)
    for c in weights:
        c.wait()
    for c in now1:
        c.wait_recv()
    place(e1, hy1[1], 1)
    place(hx1.at[1], hc1[1, 1], 1)
    lift1(slice(top, top + 2))
    edge, _ = pair1(hx - 1)
    edge_d = hx1[1] - FAR * edge
    xd1[hx] = HIGH * edge_d
    xs1[hx] = LOW * (edge - edge_d)
    lax.fori_loop(1, hx, coarse1_top, 0)
    coarse1(hx, 0, hy)

    def lines(ref, xs, ys):
        n = (xs.stop - xs.start) * (ys.stop - ys.start)
        return jnp.concatenate([ref[xs, h, ys].reshape(n, LANES) for h in range(2)], axis=1)

    chunk = hx // 2
    for i in range(2):
        rows = lines(s1s, slice(1 + i * chunk, 1 + (i + 1) * chunk), slice(PAD, PAD + hy))
        e2[4 + i * chunk : 4 + (i + 1) * chunk, PAD : PAD + hy] = times(
            rows, w1.at[:, :, 0:LANES]).reshape(chunk, hy, LANES)

    st2[...] = sums(e2[4, PAD : PAD + hy], e2[5, PAD : PAD + hy])[1]
    y_own, y_low, y_high = pl.ds(PAD, hy), pl.ds(0, PAD), pl.ds(PAD + hy, PAD)
    y_first, y_last = pl.ds(PAD, PAD), pl.ds(hy, PAD)
    own2, from2, to2 = pl.ds(4, hx), pl.ds(hx, 4), pl.ds(0, 4)
    now2 = [
        post(st2, ht2.at[y_own, :], -1, 0),
        post(e2.at[own2, y_first, :], e2.at[own2, y_high, :], 0, -1),
        post(st2.at[pl.ds(0, PAD), :], ht2.at[y_high, :], -1, -1),
    ]
    later2 = [
        post(e2.at[own2, y_last, :], e2.at[own2, y_low, :], 0, 1),
        post(e2.at[from2, y_own, :], e2.at[to2, y_own, :], 1, 0),
        post(e2.at[from2, y_last, :], e2.at[to2, y_low, :], 1, 1),
        post(e2.at[from2, y_first, :], e2.at[to2, y_high, :], 1, -1),
        post(st2.at[pl.ds(hy - PAD, PAD), :], ht2.at[y_low, :], -1, 1),
    ]

    for c in later1:
        c.wait_recv()
    place(e1, hy1[0], 0)
    place(hx1.at[1], hc1[1, 0], 0)
    place(hx1.at[0], hc1[0, 0], 0)
    place(hx1.at[0], hc1[0, 1], 1)
    first_s, first_t = pair1(0)
    first_d = first_t - FAR * hx1[0]
    xd1[0] = HIGH * first_d
    xs1[0] = LOW * (hx1[0] - first_d)
    low = slice(PAD - 2, PAD)

    lift1(low)
    edge, _ = sums(e1[cx - 2, :, low], e1[cx - 1, :, low])
    edge_d = hx1[1, :, low] - FAR * edge
    xd1[hx, :, low] = HIGH * edge_d
    xs1[hx, :, low] = LOW * (edge - edge_d)

    def cols1(src, det, smo):
        def step(n, carry):
            for h in range(2):
                load = lambda start: src[n, h, pl.ds(start, hy + 1, stride=2), :]
                s0, t0 = sums(load(PAD), load(PAD + 1))
                sm, _ = sums(load(PAD - 2), load(PAD - 1))
                d = t0 - FAR * sm
                det[n, h, 0 : hy + 1] = HIGH * d
                smo[n, h, PAD - 1 : PAD + hy] = LOW * (sm - d)
            return carry

        lax.fori_loop(0, hx + 1, step, 0)

    rows1 = hy + PAD
    parts1 = ((0, chunk), (chunk, hx + 1))

    def depth1(ref):
        magnitude = jnp.zeros((PAD, LANES), jnp.float32)
        for lo, hi in parts1:
            rows = lines(ref, slice(lo, hi), slice(0, rows1))
            if ref is s1s:
                ref[lo:hi, 1] = times(rows, w1.at[:, :, LANES : 2 * LANES]).reshape(
                    hi - lo, rows1, LANES)
                continue
            got = times(rows, w1)
            for h in range(2):
                ref[lo:hi, h] = got[:, h * LANES : (h + 1) * LANES].reshape(hi - lo, rows1, LANES)
            if ref is d1d:
                mine = got[:, LANES:].reshape(hi - lo, rows1, LANES)[:chunk, :hy]
                magnitude = magnitude + jnp.sum(
                    jnp.abs(mine).reshape(chunk * hy // PAD, PAD, LANES), axis=0)
        return magnitude

    cols1(xd1, d1d, d1s)
    part[0] = depth1(d1d)
    sums_x = [post(part.at[0], part.at[k], k, 0) for k in range(1, nx)]

    for c in now2:
        c.wait_recv()
    x2, yrows, pairs = qx + 2, qy + 2 * PAD, hy // 2 + PAD

    def lift2(rows):
        def step(n, carry):
            before, _ = sums(e2[2 * n, rows], e2[2 * n + 1, rows])
            _, part_n = sums(e2[2 * n + 2, rows], e2[2 * n + 3, rows])
            detail = part_n - FAR * before
            xd2[n, rows] = HIGH * detail
            xs2[n, rows] = LOW * (before - detail)
            return carry
        return step

    def last2(rows):
        before, _ = sums(e2[2 * x2 - 2, rows], e2[2 * x2 - 1, rows])
        detail = ht2[rows] - FAR * before
        xd2[x2 - 1, rows] = HIGH * detail
        xs2[x2 - 1, rows] = LOW * (before - detail)

    above, every = slice(PAD, hy + 2 * PAD), slice(0, hy + 2 * PAD)
    lax.fori_loop(2, x2 - 1, lift2(above), 0)
    last2(above)
    load2 = lambda start: xs2[2:x2, pl.ds(start, qy, stride=2), :]
    s0, _ = sums(load2(PAD), load2(PAD + 1))
    _, tp = sums(load2(PAD + 2), load2(PAD + 3))
    smooth2 = LOW * (s0 - (tp - FAR * s0))
    coarse2 = times(smooth2.reshape(qx * qy, LANES), w2)
    coarse2 = coarse2.reshape(qx // 2, 2, qy, LANES)
    lane = lax.broadcasted_iota(jnp.int32, (qx // 2, qy, LANES), 2)
    half = LANES // 2
    packed = jnp.where(lane < half, coarse2[:, 0], pltpu.roll(coarse2[:, 1], half, 2))
    ep3[2 : 2 + qx // 2, PAD : PAD + qy] = packed

    n_own = qx // 2
    own3 = pl.ds(2, n_own)
    z_own, z_low, z_high = pl.ds(PAD, qy), pl.ds(0, PAD), pl.ds(PAD + qy, PAD)
    z_first, z_last = pl.ds(PAD, PAD), pl.ds(qy, PAD)
    round3 = []
    for dx, xs, xd in ((1, pl.ds(n_own, 2), pl.ds(0, 2)),
                       (-1, pl.ds(2, 1), pl.ds(2 + n_own, 1)), (0, own3, own3)):
        for dy, ys, yd in ((0, z_own, z_own), (1, z_last, z_low), (-1, z_first, z_high)):
            if dx or dy:
                round3.append(post(ep3.at[xs, ys, :], ep3.at[xd, yd, :], dx, dy))

    cols1(xs1, s1d, s1s)
    depth1(d1s)

    for c in sums_x:
        c.wait_recv()
    acc = part[0]
    for k in range(1, nx):
        acc = acc + part[k]
    total[0] = acc
    sums_y = [post(total.at[0], total.at[k], 0, k) for k in range(1, ny)]

    depth1(s1d)
    depth1(s1s)

    for c in later2:
        c.wait_recv()
    lax.fori_loop(0, x2 - 1, lift2(every), 0)
    last2(every)

    def rows2(src, at):
        return forward_rows(src[at, pl.ds(0, pairs, stride=2), :],
                            src[at, pl.ds(1, pairs, stride=2), :])

    for src, det, smo in ((xd2, dd, ds), (xs2, sd, ss)):
        for band, dst in zip(rows2(src, slice(0, x2)), (det, smo)):
            dst[:, PAD // 2 : PAD // 2 + pairs] = times(
                band.reshape(x2 * pairs, LANES), w2).reshape(x2, pairs, LANES)

    for c in round3:
        c.wait_recv()
    low_s, low_t = [], []
    for n in range(n_own + 3):
        s, t = sums(ep3[n], pltpu.roll(ep3[n], half, 1))
        low_s.append(s)
        low_t.append(t)
    n3 = n_own + 2
    for n in range(n3):
        detail = low_t[n + 1] - FAR * low_s[n]
        t3d[n] = HIGH * detail
        t3s[n] = LOW * (low_s[n] - detail)
    h3 = qy // 2 + PAD
    bands = []
    for src in (t3d, t3s):
        bands += forward_rows(src[:, pl.ds(0, h3, stride=2), :], src[:, pl.ds(1, h3, stride=2), :])
    for i, band in enumerate(bands):
        bands[i] = times(band.reshape(n3 * h3, LANES), w3).reshape(n3, h3, LANES)

    for c in sums_y:
        c.wait_recv()
    acc = total[0]
    for k in range(1, ny):
        acc = acc + total[k]
    noise = jnp.sum(acc, axis=(0, 1), keepdims=True) * (math.sqrt(math.pi / 2.0) / count_all)

    lane3 = lax.broadcasted_iota(jnp.int32, (n3, h3, LANES), 2)
    noise3 = noise.reshape(1, 1, 1)
    b_dd, b_ds, b_sd = (shrink(b, noise3) for b in bands[:3])
    b_ss = jnp.where(lane3 < cz // 8, bands[3], shrink(bands[3], noise3))

    def inverse_x(det, smo):
        det, smo = det * (1.0 / HIGH), smo * (1.0 / LOW)
        one = smo + det
        even, odd = undo(det[:-1], one[1:], one[:-1])
        return weave(even, odd)

    y_d = inverse_x(b_dd, b_sd) * (1.0 / HIGH)
    y_s = inverse_x(b_ds, b_ss) * (1.0 / LOW)
    one = y_s + pltpu.roll(y_d, h3 - 1, 1)
    even, odd = undo(y_d, one, pltpu.roll(one, 1, 1))
    r2[:, pl.ds(0, h3, stride=2), :] = even
    r2[:, pl.ds(1, h3, stride=2), :] = odd
    back = times(r2[...].reshape(x2 * yrows, LANES), v3).reshape(x2, yrows, LANES)

    lane2 = lax.broadcasted_iota(jnp.int32, (x2, yrows, LANES), 2)
    ss[...] = jnp.where(lane2 < cz // 4, back, shrink(ss[...], noise3))

    def inv2(n, carry):
        def one_x(n):
            d_d = shrink(dd[n], noise) * (1.0 / HIGH)
            d_s = shrink(ds[n], noise) * (1.0 / HIGH)
            s_d = shrink(sd[n], noise) * (1.0 / LOW)
            s_s = ss[n] * (1.0 / LOW)
            return d_d, d_s, s_d + d_d, s_s + d_s

        d_d, d_s, b_d, b_s = one_x(n)
        _, _, f_d, f_s = one_x(n + 1)
        pair_d = undo(d_d, f_d, b_d)
        pair_s = undo(d_s, f_s, b_s)
        for i in range(2):
            y_d, y_s = pair_d[i] * (1.0 / HIGH), pair_s[i] * (1.0 / LOW)
            one = y_s + pltpu.roll(y_d, yrows - 1, 0)
            even, odd = undo(y_d, one, pltpu.roll(one, 1, 0))
            r1[2 * n + i, pl.ds(0, yrows, stride=2), :] = even
            r1[2 * n + i, pl.ds(1, yrows, stride=2), :] = odd
        return carry

    lax.fori_loop(0, qx + 1, inv2, 0)
    x1, y1 = hx + 2, hy + PAD
    back = times(r1[:, PAD : PAD + y1].reshape(x1 * y1, LANES), v2).reshape(x1, y1, LANES)
    s1s[:, 0] = back[1:]

    def inv1(n, carry):
        for h in range(2):
            for det, smo, dst in ((d1d, s1d, p1d), (d1s, s1s, p1s)):
                plain = smo is s1s and h == 0

                def one_x(n):
                    d = shrink(det[n, h], noise) * (1.0 / HIGH)
                    s = smo[n, h] if plain else shrink(smo[n, h], noise)
                    return d, s * (1.0 / LOW) + d

                d, before = one_x(n)
                _, one = one_x(n + 1)
                even, odd = undo(d, one, before)
                dst[2 * n, h] = even
                dst[2 * n + 1, h] = odd
        return carry

    lax.fori_loop(0, hx, inv1, 0)

    def inv1_y(n, carry):
        for h in range(2):
            y_d = p1d[n, h, 0:hy] * (1.0 / HIGH)
            y_n = p1d[n, h, 1 : hy + 1] * (1.0 / HIGH)
            s = p1s[n, h, PAD : PAD + hy] * (1.0 / LOW)
            s_b = p1s[n, h, PAD - 1 : PAD - 1 + hy] * (1.0 / LOW)
            even, odd = undo(y_d, s + y_n, s_b + y_d)
            o1[n, h, pl.ds(0, hy, stride=2), :] = even
            o1[n, h, pl.ds(1, hy, stride=2), :] = odd
        return carry

    lax.fori_loop(0, cx, inv1_y, 0)
    for c in started:
        c.wait_send()


def finish(rows_in, v1, out, ob, osem):
    cx, cy, cz = out.shape
    layers = 8
    outs = []
    for i in range(cx // layers):
        xs = slice(i * layers, (i + 1) * layers)
        rows = jnp.concatenate(
            [rows_in[xs, h].reshape(layers * cy, LANES) for h in range(2)], axis=1)
        ob[xs] = times(rows, v1).reshape(layers, cy, cz)
        c = pltpu.make_async_copy(ob.at[xs], out.at[xs], osem.at[i])
        c.start()
        outs.append(c)
    for c in outs:
        c.wait()


def on_device(nx, ny, volume):
    cx, cy, cz = volume.shape
    hx, hy, qx, qy = cx // 2, cy // 2, cx // 4, cy // 4
    n3, h3 = qx // 2 + 2, qy // 2 + PAD
    f32 = jnp.float32
    count = cx * nx * cy * ny * cz // 8
    weights = [
        halves(forward_matrix(cz), cz), halves(forward_matrix(cz // 2), LANES),
        halves(forward_matrix(cz // 4), LANES), halves(inverse_matrix(cz), cz),
        halves(inverse_matrix(cz // 2), LANES), halves(inverse_matrix(cz // 4), LANES),
    ]
    messages = 24 + nx - 1 + ny - 1
    vmem = lambda *s: pltpu.VMEM(s, f32)
    ey, ey2, ey3 = cy + 2 * PAD, hy + 2 * PAD, qy + 2 * PAD
    wide = lambda n: pltpu.VMEM((2, n, n), jnp.bfloat16)
    scratch = [
        wide(cz), wide(LANES), wide(LANES), wide(LANES), wide(LANES),
        vmem(cx, 2, ey, LANES), vmem(2, 2, ey, LANES), vmem(2, 2, cy, LANES),
        vmem(2, cx, 2, 1, LANES), vmem(2, cx, 2, 1, LANES),
        vmem(2, 2, 2, 1, LANES), vmem(2, 2, 2, 1, LANES),
        vmem(hx + 1, 2, ey, LANES), vmem(hx + 1, 2, ey, LANES),
        *[vmem(hx + 1, 2, hy + PAD, LANES) for _ in range(4)],
        vmem(hx + 4, ey2, LANES), vmem(ey2, LANES), vmem(hy, LANES),
        vmem(qx + 2, ey2, LANES), vmem(qx + 2, ey2, LANES),
        *[vmem(qx + 2, ey3, LANES) for _ in range(4)],
        vmem(qx // 2 + 3, ey3, LANES),
        vmem(n3, ey3, LANES), vmem(n3, ey3, LANES),
        vmem(qx + 2, ey3, LANES),
        vmem(hx + 2, 2 * ey3, LANES),
        vmem(cx, 2, hy + PAD, LANES), vmem(cx, 2, hy + PAD, LANES),
        vmem(nx, PAD, LANES), vmem(ny, PAD, LANES),
        pltpu.SemaphoreType.DMA((messages,)), pltpu.SemaphoreType.DMA((messages,)),
        pltpu.SemaphoreType.DMA((2,)), pltpu.SemaphoreType.DMA((6,)),
    ]
    near = pl.BlockSpec(memory_space=pltpu.VMEM)
    rows, v1 = pl.pallas_call(
        functools.partial(kernel, (cx, cy, cz), count, nx, ny),
        out_shape=(pltpu.VMEM((cx, 2, cy, LANES), f32), wide(cz)),
        in_specs=[pl.BlockSpec(memory_space=pltpu.HBM)] * 7,
        out_specs=(near, near),
        scratch_shapes=scratch,
        compiler_params=pltpu.CompilerParams(
            collective_id=0, has_side_effects=True, vmem_limit_bytes=56 * 1024 * 1024),
    )(volume, *[jnp.asarray(w) for w in weights])
    return pl.pallas_call(
        finish,
        out_shape=jax.ShapeDtypeStruct(volume.shape, f32),
        in_specs=[near, near],
        out_specs=pl.BlockSpec(memory_space=pltpu.HBM),
        scratch_shapes=[vmem(cx, cy, cz), pltpu.SemaphoreType.DMA((cx // 8,))],
        compiler_params=pltpu.CompilerParams(vmem_limit_bytes=16 * 1024 * 1024),
    )(rows, v1)


def solution(mesh):
    spec = P("gx", "gy", None)
    body = functools.partial(on_device, mesh.shape["gx"], mesh.shape["gy"])
    return jax.shard_map(body, mesh=mesh, in_specs=(spec,), out_specs=spec, check_vma=False)
```

profile of v0, /device:TPU:0, one launch (start us, length us, event | category | flops | bytes accessed | tf_op | source)
XLA Modules:
  0.0 26.0 jit_solution(14508042495764206399)
XLA Ops:
  0.0 24.0 %shard_map.73 = (f32[32,2,64,128]{3,2,1,0:T(8,128)S(1)}, bf16[2,256,256]{2,1,0:T(8,128)(2,1)S(1)}) custom-call(f32[32,64,256]{2,1,0:T(8,128)} %vol.1, bf16[2,256,256]{2,1,0:T(8,128)(2,1)} %constant.12.clone.g1, bf16[2,128,128]{2,1,0:T(8,128)(2,1)} %constant.13.clone.g2, bf16[2,128,128]{2,1,0:T(8,128)(2,1)} %constant.14.clone.g3, ...), custom_call_target="tpu_custom_call" | custom-call | tf_op jit(solution)/shard_map/pallas_call | solution.py:512
  24.0 2.0 %shard_map.74 = f32[32,64,256]{2,1,0:T(8,128)} custom-call(f32[32,2,64,128]{3,2,1,0:T(8,128)S(1)} %get-tuple-element.7.rows_in, bf16[2,256,256]{2,1,0:T(8,128)(2,1)S(1)} %get-tuple-element.8.v1), custom_call_target="tpu_custom_call" | custom-call | tf_op jit(solution)/shard_map/pallas_call | solution.py:521
where the time goes:
time: 26.2 us; the launch traced here: 26 us
  Pallas kernels  26 us (99%)
    pallas_call x1, Pallas kernels, on_device(): pl.pallas_call(functools.partial(kernel, (cx, cy, cz), count, nx, ny), ou...  24 us
    pallas_call x1, Pallas kernels, on_device(): pl.pallas_call(finish, out_shape=jax.ShapeDtypeStruct(volume.shape, f32),...  2.03 us

commit v1 on v0

v1 whole, which is shorter than its diff:
```python
import functools
import math

import jax
import jax.numpy as jnp
import numpy as np
from jax import lax
from jax.experimental import pallas as pl
from jax.experimental.pallas import tpu as pltpu
from jax.sharding import PartitionSpec as P

ROOT3 = math.sqrt(3.0)
NEAR = math.sqrt(3.0) / 4.0
FAR = (math.sqrt(3.0) - 2.0) / 4.0
LOW = (math.sqrt(3.0) - 1.0) / math.sqrt(2.0)
HIGH = (math.sqrt(3.0) + 1.0) / math.sqrt(2.0)
LANES = 128
PAD = 8


def forward_matrix(size):
    lines = np.eye(size)
    even, odd = lines[:, 0::2], lines[:, 1::2]
    smooth = even + ROOT3 * odd
    detail = odd - NEAR * smooth - FAR * np.roll(smooth, 1, 1)
    smooth = smooth - np.roll(detail, -1, 1)
    return np.concatenate([LOW * smooth, HIGH * detail], 1)


def inverse_matrix(size):
    lines = np.eye(size)
    smooth, detail = lines[:, : size // 2] / LOW, lines[:, size // 2 :] / HIGH
    first = smooth + np.roll(detail, -1, 1)
    odd = detail + NEAR * first + FAR * np.roll(first, 1, 1)
    even = first - ROOT3 * odd
    return np.stack([even, odd], 2).reshape(size, size)


def halves(matrix, size):
    full = np.zeros((size, size))
    full[: matrix.shape[0], : matrix.shape[1]] = matrix
    high = full.astype(jnp.bfloat16)
    low = (full - high.astype(np.float64)).astype(jnp.bfloat16)
    return np.stack([high, low])


def times(values, w_ref):
    high = values.astype(jnp.bfloat16)
    low = (values - high.astype(jnp.float32)).astype(jnp.bfloat16)
    dot = functools.partial(jnp.dot, preferred_element_type=jnp.float32)
    return dot(high, w_ref[0]) + (dot(low, w_ref[0]) + dot(high, w_ref[1]))


def shrink(values, noise):
    return values - jnp.clip(values, -noise, noise)


def sums(even, odd):
    smooth = even + ROOT3 * odd
    return smooth, odd - NEAR * smooth


def undo(detail, first, before):
    odd = detail + NEAR * first + FAR * before
    return first - ROOT3 * odd, odd


def weave(even, odd):
    both = jnp.stack([even, odd], axis=1)
    return both.reshape((2 * even.shape[0],) + even.shape[1:])


def forward_rows(even, odd):
    axis = even.ndim - 2
    smooth, part = sums(even, odd)
    detail = part - FAR * pltpu.roll(smooth, 1, axis)
    return detail, smooth - pltpu.roll(detail, even.shape[axis] - 1, axis)


def limits(noise, level):
    base = noise * (1.0 / LOW ** (2 * (level - 1)))
    return base * (1.0 / (HIGH * HIGH)), base * (1.0 / (HIGH * LOW)), base * (1.0 / (LOW * LOW))


def kernel(shape, nx, ny, vol, g1, gu, g3, g4, g5, g6,
           d1d, d1s, s1d, s1s, dd, ds, sd, ep3, b3, noise, v1, v2, v3,
           w1, wu, w3,
           e1, hx1, sx1, hy1, sy1, hc1, sc1, xd1, xs1,
           e2, xl, xh, xlow, xhigh, xd2, xs2, t3d, t3s,
           mine, rows_in, dummy, send, recv, lsem, wsem):
    cx, cy, cz = shape
    hx, hy, qx, qy = cx // 2, cy // 2, cx // 4, cy // 4
    ix, iy = lax.axis_index("gx"), lax.axis_index("gy")

    def device(dx, dy):
        return (lax.rem(ix + dx + nx, nx), lax.rem(iy + dy + ny, ny))

    near = [(dx, dy) for dx in (-1, 0, 1) for dy in (-1, 0, 1) if dx or dy]
    peers = [(dx, dy) for dx in range(nx) for dy in range(ny) if dx or dy]
    taken = {(dx % nx, dy % ny) for dx, dy in near}
    barrier = pltpu.get_barrier_semaphore()

    def greet(dx, dy):
        pl.semaphore_signal(barrier, inc=1, device_id=device(dx, dy),
                            device_id_type=pl.DeviceIdType.MESH)

    for d in sorted(taken):
        greet(*d)
    loads = [
        pltpu.make_async_copy(
            vol.at[:, :, pl.ds(h * LANES, LANES)],
            e1.at[:, h, pl.ds(PAD, cy), :], lsem.at[h])
        for h in range(2)
    ]
    for c in loads:
        c.start()
    for d in peers:
        if d not in taken:
            greet(*d)
    weights = [
        pltpu.make_async_copy(src, dst, wsem.at[i])
        for i, (src, dst) in enumerate(
            zip((g1, gu, g3, g4, g5, g6), (w1, wu, w3, v1, v2, v3)))
    ]
    for c in weights:
        c.start()

    sent = [0]

    def post(src, dst, dx, dy, group):
        sent[0] += math.prod(src.shape) // LANES
        pltpu.make_async_remote_copy(
            src_ref=src, dst_ref=dst, send_sem=send.at[0], recv_sem=recv.at[group],
            device_id=device(dx, dy), device_id_type=pl.DeviceIdType.MESH).start()
        return math.prod(src.shape) // LANES

    def land(sem, rows):
        part = dummy.at[pl.ds(0, rows)]
        pltpu.make_async_copy(part, part, sem).wait()

    ep3[:, 0 : PAD // 2] = jnp.zeros((qx + 4, PAD // 2, LANES), jnp.float32)
    ep3[:, PAD // 2 + hy // 2 + PAD :] = jnp.zeros((qx + 4, PAD // 2, LANES), jnp.float32)
    for ref in (dd, ds, sd):
        ref[:, 0 : PAD // 2] = jnp.zeros((qx + 2, PAD // 2, LANES), jnp.float32)
        ref[:, PAD // 2 + hy // 2 + PAD :] = jnp.zeros((qx + 2, PAD // 2, LANES), jnp.float32)

    for c in loads:
        c.wait()

    top = PAD + cy
    sx1[1] = sums(e1[0, :, PAD:top], e1[1, :, PAD:top])[1]
    sy1[1] = sums(e1[:, :, PAD : PAD + 1], e1[:, :, PAD + 1 : PAD + 2])[1]
    sx1[0] = sums(e1[cx - 2, :, PAD:top], e1[cx - 1, :, PAD:top])[0]
    sy1[0] = sums(e1[:, :, top - 2 : top - 1], e1[:, :, top - 1 : top])[0]
    for x in range(2):
        sc1[x, 1] = sums(sx1[x, :, 0:1], sx1[x, :, 1:2])[1]
        sc1[x, 0] = sums(sx1[x, :, cy - 2 : cy - 1], sx1[x, :, cy - 1 : cy])[0]
    pl.semaphore_wait(barrier, len(peers))
    step = (1, -1)
    post_x = lambda x, g: post(sx1.at[x], hx1.at[x, :, pl.ds(PAD, cy), :], step[x], 0, g)
    post_y = lambda y, g: post(sy1.at[y], hy1.at[y], 0, step[y], g)
    post_c = lambda x, y, g: post(sc1.at[x, y], hc1.at[x, y], step[x], step[y], g)
    now1 = post_c(1, 1, 0) + post_x(1, 0) + post_y(1, 0)
    later1 = (post_c(0, 1, 1) + post_c(1, 0, 1) + post_c(0, 0, 1)
              + post_x(0, 1) + post_y(0, 1))

    def place(ref, rows, side):
        if side == 0:
            ref[..., PAD - 2 : PAD - 1, :] = rows
            ref[..., PAD - 1 : PAD, :] = jnp.zeros_like(rows)
        else:
            ref[..., top : top + 1, :] = -ROOT3 * rows
            ref[..., top + 1 : top + 2, :] = rows

    def pair1(n, rows=slice(None)):
        return sums(e1[2 * n, :, rows], e1[2 * n + 1, :, rows])

    def lift1(rows):
        def step(n, carry):
            _, part_n = pair1(n, rows)
            before, _ = pair1(n - 1, rows)
            detail = part_n - FAR * before
            xd1[n, :, rows] = detail
            xs1[n, :, rows] = before - detail
            return carry

        lax.fori_loop(1, hx, step, 0)

    def coarse1(n, first, count):
        for h in range(2):
            load = lambda start: xs1[n, h, pl.ds(start + 2 * first, count, stride=2), :]
            s0, _ = sums(load(PAD), load(PAD + 1))
            _, tp = sums(load(PAD + 2), load(PAD + 3))
            s1s[n, h, PAD + first : PAD + first + count] = s0 - (tp - FAR * s0)

    def coarse1_inner(n, carry):
        coarse1(n, 0, hy)
        return carry

    def coarse1_top(n, carry):
        coarse1(n, hy - 1, 1)
        return carry

    lift1(slice(PAD, top))
    lax.fori_loop(1, hx, coarse1_inner, 0)
    for c in weights:
        c.wait()
    land(recv.at[0], now1)
    place(e1, hy1[1], 1)
    place(hx1.at[1], hc1[1, 1], 1)
    lift1(slice(top, top + 2))
    edge, _ = pair1(hx - 1)
    edge_d = hx1[1] - FAR * edge
    xd1[hx] = edge_d
    xs1[hx] = edge - edge_d
    lax.fori_loop(1, hx, coarse1_top, 0)
    coarse1(hx, 0, hy)

    def lines(ref, xs, ys):
        n = (xs.stop - xs.start) * (ys.stop - ys.start)
        return jnp.concatenate([ref[xs, h, ys].reshape(n, LANES) for h in range(2)], axis=1)

    chunk = hx // 2
    own = slice(PAD, PAD + hy)
    for i in range(2):
        rows = lines(s1s, slice(1 + i * chunk, 1 + (i + 1) * chunk), own)
        e2[i * chunk : (i + 1) * chunk, own] = times(rows, wu).reshape(chunk, hy, LANES)

    def pair2(m, rows):
        return sums(e2[2 * m, rows], e2[2 * m + 1, rows])

    def coarse2(m, rows):
        return pair2(m, rows)[0] * (1.0 + FAR) - pair2(m + 1, rows)[1]

    xl[0] = pair2(qx - 2, own)[0]
    xl[1] = e2[hx - 2, own]
    xl[2] = e2[hx - 1, own]
    xl[3] = sums(coarse2(qx - 4, own), coarse2(qx - 3, own))[0]
    xh[0] = pair2(0, own)[1]
    xh[1] = sums(coarse2(0, own), coarse2(1, own))[1]
    y_own, y_low, y_high = pl.ds(PAD, hy), pl.ds(0, PAD), pl.ds(PAD + hy, PAD)
    s_own, s_first, s_last = pl.ds(0, hy), pl.ds(0, PAD), pl.ds(hy - PAD, PAD)
    round2 = 0
    for rows_s, rows_d, dy in ((s_last, y_low, 1), (s_first, y_high, -1), (s_own, y_own, 0)):
        round2 += post(xl.at[:, rows_s, :], xlow.at[:, rows_d, :], 1, dy, 2)
        round2 += post(xh.at[:, rows_s, :], xhigh.at[:, rows_d, :], -1, dy, 2)
    round2 += post(e2.at[:, pl.ds(PAD, PAD), :], e2.at[:, y_high, :], 0, -1, 2)
    round2 += post(e2.at[:, pl.ds(hy, PAD), :], e2.at[:, y_low, :], 0, 1, 2)

    land(recv.at[1], later1)
    place(e1, hy1[0], 0)
    place(hx1.at[1], hc1[1, 0], 0)
    place(hx1.at[0], hc1[0, 0], 0)
    place(hx1.at[0], hc1[0, 1], 1)
    first_s, first_t = pair1(0)
    first_d = first_t - FAR * hx1[0]
    xd1[0] = first_d
    xs1[0] = hx1[0] - first_d
    low = slice(PAD - 2, PAD)

    lift1(low)
    edge, _ = sums(e1[cx - 2, :, low], e1[cx - 1, :, low])
    edge_d = hx1[1, :, low] - FAR * edge
    xd1[hx, :, low] = edge_d
    xs1[hx, :, low] = edge - edge_d

    def cols1(src, det, smo):
        def step(n, carry):
            for h in range(2):
                load = lambda start: src[n, h, pl.ds(start, hy + 1, stride=2), :]
                s0, t0 = sums(load(PAD), load(PAD + 1))
                sm, _ = sums(load(PAD - 2), load(PAD - 1))
                d = t0 - FAR * sm
                det[n, h, 0 : hy + 1] = d
                smo[n, h, PAD - 1 : PAD + hy] = sm - d
            return carry

        lax.fori_loop(0, hx + 1, step, 0)

    rows1 = hy + PAD
    parts1 = ((0, chunk), (chunk, hx + 1))

    def depth1(ref):
        magnitude = jnp.zeros((PAD, LANES), jnp.float32)
        for lo, hi in parts1:
            rows = lines(ref, slice(lo, hi), slice(0, rows1))
            if ref is s1s:
                ref[lo:hi, 1] = times(rows, w1.at[:, :, LANES : 2 * LANES]).reshape(
                    hi - lo, rows1, LANES)
                continue
            got = times(rows, w1)
            for h in range(2):
                ref[lo:hi, h] = got[:, h * LANES : (h + 1) * LANES].reshape(hi - lo, rows1, LANES)
            if ref is d1d:
                inside = got[:, LANES:].reshape(hi - lo, rows1, LANES)[:chunk, :hy]
                magnitude = magnitude + jnp.sum(
                    jnp.abs(inside).reshape(chunk * hy // PAD, PAD, LANES), axis=0)
        return magnitude

    cols1(xd1, d1d, d1s)
    mine[...] = jnp.sum(depth1(d1d), axis=0, keepdims=True)
    landed = 0
    for k, d in enumerate(peers):
        landed += post(mine, rows_in.at[k], d[0], d[1], 3)

    cols1(xs1, s1d, s1s)
    depth1(d1s)
    depth1(s1d)
    depth1(s1s)

    land(recv.at[2], round2)
    every = slice(0, hy + 2 * PAD)
    before = xlow[0]
    xs2[0] = xlow[3]
    for m in range(-1, qx + 1):
        if m == qx:
            smooth, part = None, xhigh[0]
        elif m == -1:
            smooth, part = sums(xlow[1], xlow[2])
        else:
            smooth, part = pair2(m, every)
        detail = part - FAR * before
        xd2[m + 1] = detail
        xs2[m + 2] = before - detail
        before = smooth
    xs2[qx + 3] = xhigh[1]
    pairs = hy // 2 + PAD

    def rows2(src):
        return forward_rows(src[:, pl.ds(0, pairs, stride=2), :],
                            src[:, pl.ds(1, pairs, stride=2), :])

    mid = slice(PAD // 2, PAD // 2 + pairs)
    dd[:, mid], ds[:, mid] = rows2(xd2)
    det, smo = rows2(xs2)
    sd[:, mid] = det[1 : qx + 3]
    ep3[:, mid] = smo

    n_own, n3, h3 = qx // 2, qx // 2 + 2, qy // 2 + PAD
    low_s, low_t = [ep3[0]], [None]
    for n in range(n_own + 1):
        s, t = sums(ep3[1 + 2 * n], ep3[2 + 2 * n])
        low_s.append(s)
        low_t.append(t)
    low_t.append(ep3[qx + 3])
    for n in range(n3):
        detail = low_t[n + 1] - FAR * low_s[n]
        t3d[n] = detail
        t3s[n] = low_s[n] - detail
    bands = []
    for src in (t3d, t3s):
        bands += forward_rows(src[:, pl.ds(0, h3, stride=2), :], src[:, pl.ds(1, h3, stride=2), :])
    for i, band in enumerate(bands):
        b3[i] = times(band.reshape(n3 * h3, LANES), w3).reshape(n3, h3, LANES)

    land(recv.at[3], landed)
    acc = mine[...]
    for k in range(len(peers)):
        acc = acc + rows_in[k]
    noise[...] = acc
    land(send.at[0], sent[0])


def finish(shape, count_all, d1d, d1s, s1d, s1s, dd, ds, sd, ep3, b3, total, v1, v2, v3, out,
           ss, r2, r1, s0, p1d, p1s, o1, ob, osem):
    cx, cy, cz = shape
    hx, hy, qx, qy = cx // 2, cy // 2, cx // 4, cy // 4
    n3, h3, x2, yrows = qx // 2 + 2, qy // 2 + PAD, qx + 2, qy + 2 * PAD
    noise = jnp.sum(total[...], axis=(0, 1), keepdims=True) * (
        HIGH * HIGH * math.sqrt(math.pi / 2.0) / count_all)

    far1, mid1, near1 = limits(noise, 1)

    def inv1(det, smo, h, dst, limit_d, limit_s):
        def one_x(n):
            d = shrink(det[n, h], limit_d)
            s = s0[n] if limit_s is None else shrink(smo[n, h], limit_s)
            return d, s + d

        def step(n, carry):
            d, before = carry
            after, one = one_x(n + 1)
            even, odd = undo(d, one, before)
            dst[2 * n, h] = even
            dst[2 * n + 1, h] = odd
            return after, one

        lax.fori_loop(0, hx, step, one_x(0), unroll=4)

    for h in range(2):
        inv1(d1d, s1d, h, p1d, far1, mid1)
    inv1(d1s, s1s, 1, p1s, mid1, near1)

    far3, mid3, near3 = (v.reshape(1, 1, 1) for v in limits(noise, 3))
    lane3 = lax.broadcasted_iota(jnp.int32, (n3, h3, LANES), 2)
    b_dd, b_ds, b_sd = shrink(b3[0], far3), shrink(b3[1], mid3), shrink(b3[2], mid3)
    b_ss = jnp.where(lane3 < cz // 8, b3[3], shrink(b3[3], near3))

    def inverse_x(det, smo):
        one = smo + det
        even, odd = undo(det[:-1], one[1:], one[:-1])
        return weave(even, odd)

    y_d = inverse_x(b_dd, b_sd)
    y_s = inverse_x(b_ds, b_ss)
    one = y_s + pltpu.roll(y_d, h3 - 1, 1)
    even, odd = undo(y_d, one, pltpu.roll(one, 1, 1))
    r2[:, pl.ds(0, h3, stride=2), :] = even
    r2[:, pl.ds(1, h3, stride=2), :] = odd
    back = times(r2[...].reshape(x2 * yrows, LANES), v3).reshape(x2, yrows, LANES)

    far2, mid2, near2 = limits(noise, 2)
    lane2 = lax.broadcasted_iota(jnp.int32, (x2, yrows, LANES), 2)
    ss[...] = jnp.where(lane2 < cz // 4, back, shrink(ep3[1 : qx + 3], near2.reshape(1, 1, 1)))

    def one_x(n):
        d_d = shrink(dd[n], far2)
        d_s = shrink(ds[n], mid2)
        s_d = shrink(sd[n], mid2)
        return d_d, d_s, s_d + d_d, ss[n] + d_s

    def inv2(n, carry):
        d_d, d_s, b_d, b_s = carry
        after = one_x(n + 1)
        pair_d = undo(d_d, after[2], b_d)
        pair_s = undo(d_s, after[3], b_s)
        for i in range(2):
            y_d, y_s = pair_d[i], pair_s[i]
            one = y_s + pltpu.roll(y_d, yrows - 1, 0)
            even, odd = undo(y_d, one, pltpu.roll(one, 1, 0))
            r1[2 * n + i, pl.ds(0, yrows, stride=2), :] = even
            r1[2 * n + i, pl.ds(1, yrows, stride=2), :] = odd
        return after

    lax.fori_loop(0, qx + 1, inv2, one_x(0), unroll=3)
    x1, y1 = hx + 2, hy + PAD
    back = times(r1[:, PAD : PAD + y1].reshape(x1 * y1, LANES), v2).reshape(x1, y1, LANES)
    s0[...] = back[1:]
    inv1(d1s, s1s, 0, p1s, mid1, None)

    def inv1_y(n):
        for h in range(2):
            y_d = p1d[n, h, 0:hy]
            y_n = p1d[n, h, 1 : hy + 1]
            s = p1s[n, h, PAD : PAD + hy]
            s_b = p1s[n, h, PAD - 1 : PAD - 1 + hy]
            even, odd = undo(y_d, s + y_n, s_b + y_d)
            o1[n, h, pl.ds(0, hy, stride=2), :] = even
            o1[n, h, pl.ds(1, hy, stride=2), :] = odd

    layers = 8
    outs = []
    for n in range(layers):
        inv1_y(n)
    for i in range(cx // layers):
        for n in range((i + 1) * layers, min((i + 2) * layers, cx)):
            inv1_y(n)
        xs = slice(i * layers, (i + 1) * layers)
        rows = jnp.concatenate(
            [o1[xs, h].reshape(layers * cy, LANES) for h in range(2)], axis=1)
        ob[xs] = times(rows, v1).reshape(layers, cy, cz)
        c = pltpu.make_async_copy(ob.at[xs], out.at[xs], osem.at[i])
        c.start()
        outs.append(c)
    for c in outs:
        c.wait()


def on_device(nx, ny, volume):
    cx, cy, cz = volume.shape
    hx, hy, qx, qy = cx // 2, cy // 2, cx // 4, cy // 4
    n3, h3 = qx // 2 + 2, qy // 2 + PAD
    f32 = jnp.float32
    count = cx * nx * cy * ny * cz // 8
    w1 = forward_matrix(cz)
    weights = [
        halves(w1, cz), halves(w1[:, : cz // 2] @ forward_matrix(cz // 2), cz)[:, :, : cz // 2],
        halves(forward_matrix(cz // 4), LANES), halves(inverse_matrix(cz), cz),
        halves(inverse_matrix(cz // 2), LANES), halves(inverse_matrix(cz // 4), LANES),
    ]
    vmem = lambda *s: pltpu.VMEM(s, f32)
    ey, ey2, ey3 = cy + 2 * PAD, hy + 2 * PAD, qy + 2 * PAD
    wide = lambda *s: pltpu.VMEM((2,) + s, jnp.bfloat16)
    made = (
        *[vmem(hx + 1, 2, hy + PAD, LANES) for _ in range(4)],
        *[vmem(qx + 2, ey3, LANES) for _ in range(3)],
        vmem(qx + 4, ey3, LANES), vmem(4, n3, h3, LANES), vmem(1, LANES),
        wide(cz, cz), wide(LANES, LANES), wide(LANES, LANES),
    )
    rows = 4 * cy + 4 * cx + 8 + 6 * (hy + 2 * PAD) + 2 * hx * PAD + nx * ny
    scratch = [
        wide(cz, cz), wide(cz, LANES), wide(LANES, LANES),
        vmem(cx, 2, ey, LANES), vmem(2, 2, ey, LANES), vmem(2, 2, cy, LANES),
        vmem(2, cx, 2, 1, LANES), vmem(2, cx, 2, 1, LANES),
        vmem(2, 2, 2, 1, LANES), vmem(2, 2, 2, 1, LANES),
        vmem(hx + 1, 2, ey, LANES), vmem(hx + 1, 2, ey, LANES),
        vmem(hx, ey2, LANES), vmem(4, hy, LANES), vmem(2, hy, LANES),
        vmem(4, ey2, LANES), vmem(2, ey2, LANES),
        vmem(qx + 2, ey2, LANES), vmem(qx + 4, ey2, LANES),
        vmem(n3, ey3, LANES), vmem(n3, ey3, LANES),
        vmem(1, LANES), vmem(nx * ny - 1, 1, LANES), vmem(rows, 1, LANES),
        pltpu.SemaphoreType.DMA((1,)), pltpu.SemaphoreType.DMA((4,)),
        pltpu.SemaphoreType.DMA((2,)), pltpu.SemaphoreType.DMA((6,)),
    ]
    near = pl.BlockSpec(memory_space=pltpu.VMEM)
    passed = pl.pallas_call(
        functools.partial(kernel, (cx, cy, cz), nx, ny),
        out_shape=made,
        in_specs=[pl.BlockSpec(memory_space=pltpu.HBM)] * 7,
        out_specs=(near,) * len(made),
        scratch_shapes=scratch,
        compiler_params=pltpu.CompilerParams(
            collective_id=0, has_side_effects=True, vmem_limit_bytes=40 * 1024 * 1024),
    )(volume, *[jnp.asarray(w) for w in weights])
    return pl.pallas_call(
        functools.partial(finish, (cx, cy, cz), count),
        out_shape=jax.ShapeDtypeStruct(volume.shape, f32),
        in_specs=[near] * len(made),
        out_specs=pl.BlockSpec(memory_space=pltpu.HBM),
        scratch_shapes=[
            vmem(qx + 2, ey3, LANES), vmem(qx + 2, ey3, LANES), vmem(hx + 2, 2 * ey3, LANES),
            vmem(hx + 1, hy + PAD, LANES),
            vmem(cx, 2, hy + PAD, LANES), vmem(cx, 2, hy + PAD, LANES),
            vmem(cx, 2, cy, LANES), vmem(cx, cy, cz), pltpu.SemaphoreType.DMA((cx // 8,)),
        ],
        compiler_params=pltpu.CompilerParams(vmem_limit_bytes=24 * 1024 * 1024),
    )(*passed)


def solution(mesh):
    spec = P("gx", "gy", None)
    body = functools.partial(on_device, mesh.shape["gx"], mesh.shape["gy"])
    return jax.shard_map(body, mesh=mesh, in_specs=(spec,), out_specs=spec, check_vma=False)
```

time: 26.2 us -> 29.1 us (1.11)
  local copies, waits for them, and re-layouts: 0 us -> 6.91 us
  Pallas kernels: 26 us -> 21.8 us
    unnamed x0 -> x14, local copies, waits for them, and re-layouts: none -> 6.91 us
    pallas_call x2, Pallas kernels: 26 us -> 21.8 us  [the longest x1 17.7 us: on_device(): pl.pallas_call(functools.partial(kernel, (cx, cy, cz), nx, ny), out_shape...]
where the time goes in v1:
time: 29.1 us; the launch traced here: 28.7 us
  Pallas kernels  21.8 us (75%)
  local copies, waits for them, and re-layouts  6.91 us (24%)
    pallas_call x1, Pallas kernels, on_device(): pl.pallas_call(functools.partial(kernel, (cx, cy, cz), nx, ny), out_shape...  17.7 us
    unnamed x14, local copies, waits for them, and re-layouts  6.91 us
    pallas_call x1, Pallas kernels, on_device(): pl.pallas_call(functools.partial(finish, (cx, cy, cz), count), out_shape=...  4.15 us

profile of v1, /device:TPU:0, one launch (start us, length us, event | category | flops | bytes accessed | tf_op | source)
XLA Modules:
  0.0 28.7 jit_solution(13124146536568452001)
XLA Ops:
  0.0 0.0 copy-start
  0.0 1.6 %copy-done = f32[32,64,256]{2,1,0:T(8,128)S(1)} copy-done((f32[32,64,256]{2,1,0:T(8,128)S(1)}, f32[32,64,256]{2,1,0:T(8,128)}, u32[]{:S(2)}) %copy-start) | copy-done | bytes 2097176
  1.6 0.0 copy-start.1
  1.6 0.9 %copy-done.1 = bf16[2,256,256]{2,1,0:T(8,128)(2,1)S(1)} copy-done((bf16[2,256,256]{2,1,0:T(8,128)(2,1)S(1)}, bf16[2,256,256]{2,1,0:T(8,128)(2,1)}, u32[]{:S(2)}) %copy-start.1) | copy-done | bytes 262168
  2.5 0.0 copy-start.2
  2.5 0.9 %copy-done.2 = bf16[2,256,256]{2,1,0:T(8,128)(2,1)S(1)} copy-done((bf16[2,256,256]{2,1,0:T(8,128)(2,1)S(1)}, bf16[2,256,256]{2,1,0:T(8,128)(2,1)}, u32[]{:S(2)}) %copy-start.2) | copy-done | bytes 262168
  3.5 0.0 copy-start.3
  3.5 0.9 %copy-done.3 = bf16[2,256,128]{2,1,0:T(8,128)(2,1)S(1)} copy-done((bf16[2,256,128]{2,1,0:T(8,128)(2,1)S(1)}, bf16[2,256,128]{2,1,0:T(8,128)(2,1)}, u32[]{:S(2)}) %copy-start.3) | copy-done | bytes 131096
  4.4 0.0 copy-start.4
  4.4 0.8 %copy-done.4 = bf16[2,128,128]{2,1,0:T(8,128)(2,1)S(1)} copy-done((bf16[2,128,128]{2,1,0:T(8,128)(2,1)S(1)}, bf16[2,128,128]{2,1,0:T(8,128)(2,1)}, u32[]{:S(2)}) %copy-start.4) | copy-done | bytes 65560
  5.2 0.0 copy-start.5
  5.2 0.8 %copy-done.5 = bf16[2,128,128]{2,1,0:T(8,128)(2,1)S(1)} copy-done((bf16[2,128,128]{2,1,0:T(8,128)(2,1)S(1)}, bf16[2,128,128]{2,1,0:T(8,128)(2,1)}, u32[]{:S(2)}) %copy-start.5) | copy-done | bytes 65560
  6.1 0.0 copy-start.6
  6.1 0.8 %copy-done.6 = bf16[2,128,128]{2,1,0:T(8,128)(2,1)S(1)} copy-done((bf16[2,128,128]{2,1,0:T(8,128)(2,1)S(1)}, bf16[2,128,128]{2,1,0:T(8,128)(2,1)}, u32[]{:S(2)}) %copy-start.6) | copy-done | bytes 65560
  6.9 17.7 %shard_map.73 = (f32[17,2,40,128]{3,2,1,0:T(8,128)S(1)}, f32[17,2,40,128]{3,2,1,0:T(8,128)S(1)}, f32[17,2,40,128]{3,2,1,0:T(8,128)S(1)}, f32[17,2,40,128]{3,2,1,...) custom-call(f32[32,64,256]{2,1,0:T(8,128)S(1)} %copy-done, ...), custom_call_target="tpu_custom_call" | custom-call | tf_op jit(solution)/shard_map/pallas_call | solution.py:506
  24.6 4.1 %shard_map.74 = f32[32,64,256]{2,1,0:T(8,128)} custom-call(f32[17,2,40,128]{3,2,1,0:T(8,128)S(1)} %get-tuple-element.18.d1d, f32[17,2,40,128]{3,2,1,0:T(8,128)S(1)} %get-tuple-element.19.d1s, f32[17,2,40,128]{3,2,1,0:T(8,128)S(1)} %get-tuple-element.20.s1d, f32[17,2,40,128]{3,2,1,0:T(8,128)S(1)} %get-tuple-element.21.s1s, ...), custom_call_target="tpu_custom_call" | custom-call | tf_op jit(solution)/shard_map/pallas_call | solution.py:515
Async XLA Ops:
  0.0 1.6 %copy-start = (f32[32,64,256]{2,1,0:T(8,128)S(1)}, f32[32,64,256]{2,1,0:T(8,128)}, u32[]{:S(2)}) copy-start(f32[32,64,256]{2,1,0:T(8,128)} %vol.1) | copy-start | bytes 6291460
  1.6 0.9 %copy-start.1 = (bf16[2,256,256]{2,1,0:T(8,128)(2,1)S(1)}, bf16[2,256,256]{2,1,0:T(8,128)(2,1)}, u32[]{:S(2)}) copy-start(bf16[2,256,256]{2,1,0:T(8,128)(2,1)} %constant.15.clone.g4) | copy-start | bytes 786436
  2.5 0.9 %copy-start.2 = (bf16[2,256,256]{2,1,0:T(8,128)(2,1)S(1)}, bf16[2,256,256]{2,1,0:T(8,128)(2,1)}, u32[]{:S(2)}) copy-start(bf16[2,256,256]{2,1,0:T(8,128)(2,1)} %constant.12.clone.g1) | copy-start | bytes 786436
  3.5 0.9 %copy-start.3 = (bf16[2,256,128]{2,1,0:T(8,128)(2,1)S(1)}, bf16[2,256,128]{2,1,0:T(8,128)(2,1)}, u32[]{:S(2)}) copy-start(bf16[2,256,128]{2,1,0:T(8,128)(2,1)} %constant.13.clone.gu) | copy-start | bytes 393220
  4.4 0.8 %copy-start.4 = (bf16[2,128,128]{2,1,0:T(8,128)(2,1)S(1)}, bf16[2,128,128]{2,1,0:T(8,128)(2,1)}, u32[]{:S(2)}) copy-start(bf16[2,128,128]{2,1,0:T(8,128)(2,1)} %constant.17.clone.g6) | copy-start | bytes 196612
  5.2 0.8 %copy-start.5 = (bf16[2,128,128]{2,1,0:T(8,128)(2,1)S(1)}, bf16[2,128,128]{2,1,0:T(8,128)(2,1)}, u32[]{:S(2)}) copy-start(bf16[2,128,128]{2,1,0:T(8,128)(2,1)} %constant.16.clone.g5) | copy-start | bytes 196612
  6.1 0.8 %copy-start.6 = (bf16[2,128,128]{2,1,0:T(8,128)(2,1)S(1)}, bf16[2,128,128]{2,1,0:T(8,128)(2,1)}, u32[]{:S(2)}) copy-start(bf16[2,128,128]{2,1,0:T(8,128)(2,1)} %constant.14.clone.g3) | copy-start | bytes 196612

commit v2 on v1

--- a/solution.py
+++ b/solution.py
@@ -510,7 +510,7 @@
         out_specs=(near,) * len(made),
         scratch_shapes=scratch,
         compiler_params=pltpu.CompilerParams(
-            collective_id=0, has_side_effects=True, vmem_limit_bytes=40 * 1024 * 1024),
+            collective_id=0, has_side_effects=True, vmem_limit_bytes=56 * 1024 * 1024),
     )(volume, *[jnp.asarray(w) for w in weights])
     return pl.pallas_call(
         functools.partial(finish, (cx, cy, cz), count),

time: 29.1 us -> 21.9 us (0.75)
  local copies, waits for them, and re-layouts: 6.91 us -> 0 us
    unnamed x14 -> x0, local copies, waits for them, and re-layouts: 6.91 us -> none
where the time goes in v2:
time: 21.9 us; the launch traced here: 21.7 us
  Pallas kernels  21.7 us (99%)
    pallas_call x1, Pallas kernels, on_device(): pl.pallas_call(functools.partial(kernel, (cx, cy, cz), nx, ny), out_shape...  17.6 us
    pallas_call x1, Pallas kernels, on_device(): pl.pallas_call(functools.partial(finish, (cx, cy, cz), count), out_shape=...  4.14 us

profile of v2, /device:TPU:0, one launch (start us, length us, event | category | flops | bytes accessed | tf_op | source)
XLA Modules:
  0.0 21.7 jit_solution(15390089013653550207)
XLA Ops:
  0.0 17.6 %shard_map.73 = (f32[17,2,40,128]{3,2,1,0:T(8,128)S(1)}, f32[17,2,40,128]{3,2,1,0:T(8,128)S(1)}, f32[17,2,40,128]{3,2,1,0:T(8,128)S(1)}, f32[17,2,40,128]{3,2,1,...) custom-call(f32[32,64,256]{2,1,0:T(8,128)} %vol.1, ...), custom_call_target="tpu_custom_call" | custom-call | tf_op jit(solution)/shard_map/pallas_call | solution.py:506
  17.6 4.1 %shard_map.74 = f32[32,64,256]{2,1,0:T(8,128)} custom-call(f32[17,2,40,128]{3,2,1,0:T(8,128)S(1)} %get-tuple-element.18.d1d, f32[17,2,40,128]{3,2,1,0:T(8,128)S(1)} %get-tuple-element.19.d1s, f32[17,2,40,128]{3,2,1,0:T(8,128)S(1)} %get-tuple-element.20.s1d, f32[17,2,40,128]{3,2,1,0:T(8,128)S(1)} %get-tuple-element.21.s1s, ...), custom_call_target="tpu_custom_call" | custom-call | tf_op jit(solution)/shard_map/pallas_call | solution.py:515

commit v3 on v2

--- a/solution.py
+++ b/solution.py
@@ -82,9 +82,9 @@
     return base * (1.0 / (HIGH * HIGH)), base * (1.0 / (HIGH * LOW)), base * (1.0 / (LOW * LOW))
 
 
-def kernel(shape, nx, ny, vol, g1, gu, g3, g4, g5, g6,
+def kernel(shape, nx, ny, vol, g1, g2, g3, g4, g5, g6,
            d1d, d1s, s1d, s1s, dd, ds, sd, ep3, b3, noise, v1, v2, v3,
-           w1, wu, w3,
+           w1, w2, w3,
            e1, hx1, sx1, hy1, sy1, hc1, sc1, xd1, xs1,
            e2, xl, xh, xlow, xhigh, xd2, xs2, t3d, t3s,
            mine, rows_in, dummy, send, recv, lsem, wsem):
@@ -117,13 +117,11 @@
     for d in peers:
         if d not in taken:
             greet(*d)
-    weights = [
-        pltpu.make_async_copy(src, dst, wsem.at[i])
-        for i, (src, dst) in enumerate(
-            zip((g1, gu, g3, g4, g5, g6), (w1, wu, w3, v1, v2, v3)))
-    ]
-    for c in weights:
-        c.start()
+    first_weight = pltpu.make_async_copy(g1, w1, wsem.at[0])
+    first_weight.start()
+    more = list(zip((g2, g3, g4, g5, g6), (w2, w3, v1, v2, v3)))
+    for src, dst in more:
+        pltpu.make_async_copy(src, dst, wsem.at[1]).start()
 
     sent = [0]
 
@@ -144,33 +142,49 @@
         ref[:, 0 : PAD // 2] = jnp.zeros((qx + 2, PAD // 2, LANES), jnp.float32)
         ref[:, PAD // 2 + hy // 2 + PAD :] = jnp.zeros((qx + 2, PAD // 2, LANES), jnp.float32)
 
+    top = PAD + cy
+    own1, own = slice(PAD, top), slice(PAD, PAD + hy)
     for c in loads:
         c.wait()
-
-    top = PAD + cy
-    sx1[1] = sums(e1[0, :, PAD:top], e1[1, :, PAD:top])[1]
+    first_weight.wait()
+
+    def depth(xs, ys):
+        shape = (xs.stop - xs.start, ys.stop - ys.start, LANES)
+        rows = jnp.concatenate(
+            [e1[xs, h, ys].reshape(shape[0] * shape[1], LANES) for h in range(2)], axis=1)
+        got = times(rows, w1)
+        for h in range(2):
+            e1[xs, h, ys] = got[:, h * LANES : (h + 1) * LANES].reshape(shape)
+
+    inner = slice(2 * PAD, top - PAD)
+    depth(slice(0, cx), slice(PAD, 2 * PAD))
+    depth(slice(0, cx), slice(top - PAD, top))
+    depth(slice(0, 2), inner)
+    depth(slice(cx - 2, cx), inner)
+    sx1[1] = sums(e1[0, :, own1], e1[1, :, own1])[1]
+    sx1[0] = sums(e1[cx - 2, :, own1], e1[cx - 1, :, own1])[0]
     sy1[1] = sums(e1[:, :, PAD : PAD + 1], e1[:, :, PAD + 1 : PAD + 2])[1]
-    sx1[0] = sums(e1[cx - 2, :, PAD:top], e1[cx - 1, :, PAD:top])[0]
     sy1[0] = sums(e1[:, :, top - 2 : top - 1], e1[:, :, top - 1 : top])[0]
     for x in range(2):
         sc1[x, 1] = sums(sx1[x, :, 0:1], sx1[x, :, 1:2])[1]
         sc1[x, 0] = sums(sx1[x, :, cy - 2 : cy - 1], sx1[x, :, cy - 1 : cy])[0]
     pl.semaphore_wait(barrier, len(peers))
     step = (1, -1)
-    post_x = lambda x, g: post(sx1.at[x], hx1.at[x, :, pl.ds(PAD, cy), :], step[x], 0, g)
-    post_y = lambda y, g: post(sy1.at[y], hy1.at[y], 0, step[y], g)
-    post_c = lambda x, y, g: post(sc1.at[x, y], hc1.at[x, y], step[x], step[y], g)
-    now1 = post_c(1, 1, 0) + post_x(1, 0) + post_y(1, 0)
-    later1 = (post_c(0, 1, 1) + post_c(1, 0, 1) + post_c(0, 0, 1)
-              + post_x(0, 1) + post_y(0, 1))
-
-    def place(ref, rows, side):
-        if side == 0:
-            ref[..., PAD - 2 : PAD - 1, :] = rows
-            ref[..., PAD - 1 : PAD, :] = jnp.zeros_like(rows)
-        else:
-            ref[..., top : top + 1, :] = -ROOT3 * rows
-            ref[..., top + 1 : top + 2, :] = rows
+    post_x = lambda x, h, g: post(
+        sx1.at[x, h], hx1.at[x, h, pl.ds(PAD, cy), :], step[x], 0, g)
+    post_y = lambda y, h, g: post(sy1.at[y, :, h], hy1.at[y, :, h], 0, step[y], g)
+    post_c = lambda x, y, h, g: post(
+        sc1.at[x, y, h], hc1.at[x, y, h], step[x], step[y], g)
+    noise1 = post_c(0, 0, 1, 0) + post_x(0, 1, 0) + post_y(0, 1, 0)
+    coarse1 = post_c(1, 1, 0, 1) + post_x(1, 0, 1) + post_y(1, 0, 1)
+    later1 = (post_c(0, 0, 0, 2) + post_c(1, 1, 1, 2) + post_x(0, 0, 2) + post_x(1, 1, 2)
+              + post_y(0, 0, 2) + post_y(1, 1, 2))
+    for h in range(2):
+        later1 += post_c(0, 1, h, 2) + post_c(1, 0, h, 2)
+
+    slab = 4
+    for lo in range(2, cx - 2, slab):
+        depth(slice(lo, min(lo + slab, cx - 2)), inner)
 
     def pair1(n, rows=slice(None)):
         return sums(e1[2 * n, :, rows], e1[2 * n + 1, :, rows])
@@ -186,45 +200,64 @@
 
         lax.fori_loop(1, hx, step, 0)
 
-    def coarse1(n, first, count):
-        for h in range(2):
-            load = lambda start: xs1[n, h, pl.ds(start + 2 * first, count, stride=2), :]
-            s0, _ = sums(load(PAD), load(PAD + 1))
-            _, tp = sums(load(PAD + 2), load(PAD + 3))
-            s1s[n, h, PAD + first : PAD + first + count] = s0 - (tp - FAR * s0)
-
-    def coarse1_inner(n, carry):
-        coarse1(n, 0, hy)
-        return carry
-
-    def coarse1_top(n, carry):
-        coarse1(n, hy - 1, 1)
-        return carry
-
-    lift1(slice(PAD, top))
-    lax.fori_loop(1, hx, coarse1_inner, 0)
-    for c in weights:
-        c.wait()
-    land(recv.at[0], now1)
-    place(e1, hy1[1], 1)
-    place(hx1.at[1], hc1[1, 1], 1)
-    lift1(slice(top, top + 2))
-    edge, _ = pair1(hx - 1)
-    edge_d = hx1[1] - FAR * edge
-    xd1[hx] = edge_d
-    xs1[hx] = edge - edge_d
-    lax.fori_loop(1, hx, coarse1_top, 0)
-    coarse1(hx, 0, hy)
-
-    def lines(ref, xs, ys):
-        n = (xs.stop - xs.start) * (ys.stop - ys.start)
-        return jnp.concatenate([ref[xs, h, ys].reshape(n, LANES) for h in range(2)], axis=1)
-
-    chunk = hx // 2
-    own = slice(PAD, PAD + hy)
-    for i in range(2):
-        rows = lines(s1s, slice(1 + i * chunk, 1 + (i + 1) * chunk), own)
-        e2[i * chunk : (i + 1) * chunk, own] = times(rows, wu).reshape(chunk, hy, LANES)
+    def shrunk(n):
+        load = lambda start: xs1[n, 0, pl.ds(start, hy, stride=2), :]
+        s0, _ = sums(load(PAD), load(PAD + 1))
+        _, tp = sums(load(PAD + 2), load(PAD + 3))
+        s1s[n, 0, own] = s0 - (tp - FAR * s0)
+
+    def finest(n):
+        load = lambda start: xd1[n, 1, pl.ds(start, hy, stride=2), :]
+        _, t0 = sums(load(PAD), load(PAD + 1))
+        sm, _ = sums(load(PAD - 2), load(PAD - 1))
+        return jnp.abs(t0 - FAR * sm)
+
+    def fold(values):
+        return jnp.sum(values.reshape(hy // PAD, PAD, LANES), axis=0)
+
+    known = lax.broadcasted_iota(jnp.int32, (hy, LANES), 0) > 0
+
+    def inside(n, magnitude):
+        shrunk(n)
+        return magnitude + fold(jnp.where(known, finest(n), 0.0))
+
+    lift1(own1)
+    magnitude = lax.fori_loop(1, hx, inside, jnp.zeros((PAD, LANES), jnp.float32))
+    land(wsem.at[1], sum(2 * math.prod(dst.shape) // (4 * LANES) for _, dst in more))
+    done = hy - PAD
+    rows = s1s[1:hx, 0, PAD : PAD + done].reshape((hx - 1) * done, LANES)
+    e2[0 : hx - 1, PAD : PAD + done] = times(rows, w2).reshape(hx - 1, done, LANES)
+
+    land(recv.at[0], noise1)
+    edge = hy1[0, :, 1].reshape(hx, 2, 1, LANES)
+    edge_s, edge_t = sums(edge[:, 0], edge[:, 1])
+    edge_d = edge_t - FAR * jnp.concatenate([hc1[0, 0, 1][None], edge_s[:-1]], axis=0)
+    xd1[0, 1, own1] = sums(e1[0, 1, own1], e1[1, 1, own1])[1] - FAR * hx1[0, 1, own1]
+    xd1[0, 1, PAD - 2 : PAD - 1] = edge_d[0]
+    xd1[0, 1, PAD - 1 : PAD] = jnp.zeros((1, LANES), jnp.float32)
+    _, edge_t = sums(xd1[1:hx, 1, PAD : PAD + 1], xd1[1:hx, 1, PAD + 1 : PAD + 2])
+    row = jnp.sum(jnp.abs(edge_t - FAR * edge_d[1:]), axis=0)
+    mine[...] = row + jnp.sum(magnitude + fold(finest(0)), axis=0, keepdims=True)
+    landed = 0
+    for k, d in enumerate(peers):
+        landed += post(mine, rows_in.at[k], d[0], d[1], 4)
+
+    land(recv.at[1], coarse1)
+    edge, _ = sums(e1[cx - 2, 0, own1], e1[cx - 1, 0, own1])
+    xs1[hx, 0, own1] = edge - (hx1[1, 0, own1] - FAR * edge)
+    shrunk(hx)
+    edge = hy1[1, :, 0].reshape(hx, 2, 1, LANES)
+    edge_s, edge_t = sums(edge[:, 0], edge[:, 1])
+    after = jnp.concatenate([edge_t[1:], hc1[1, 1, 0][None]], axis=0)
+    last_t = edge_s - (after - FAR * edge_s)
+    last_s, _ = sums(xs1[1 : hx + 1, 0, top - 2 : top - 1], xs1[1 : hx + 1, 0, top - 1 : top])
+    s1s[1 : hx + 1, 0, PAD + hy - 1 : PAD + hy] = last_s - (last_t - FAR * last_s)
+    rows = jnp.concatenate(
+        [s1s[1:hx, 0, PAD + done : PAD + hy].reshape((hx - 1) * PAD, LANES), s1s[hx, 0, own]],
+        axis=0)
+    got = times(rows, w2)
+    e2[0 : hx - 1, PAD + done : PAD + hy] = got[: (hx - 1) * PAD].reshape(hx - 1, PAD, LANES)
+    e2[hx - 1, own] = got[(hx - 1) * PAD :]
 
     def pair2(m, rows):
         return sums(e2[2 * m, rows], e2[2 * m + 1, rows])
@@ -242,27 +275,36 @@
     s_own, s_first, s_last = pl.ds(0, hy), pl.ds(0, PAD), pl.ds(hy - PAD, PAD)
     round2 = 0
     for rows_s, rows_d, dy in ((s_last, y_low, 1), (s_first, y_high, -1), (s_own, y_own, 0)):
-        round2 += post(xl.at[:, rows_s, :], xlow.at[:, rows_d, :], 1, dy, 2)
-        round2 += post(xh.at[:, rows_s, :], xhigh.at[:, rows_d, :], -1, dy, 2)
-    round2 += post(e2.at[:, pl.ds(PAD, PAD), :], e2.at[:, y_high, :], 0, -1, 2)
-    round2 += post(e2.at[:, pl.ds(hy, PAD), :], e2.at[:, y_low, :], 0, 1, 2)
-
-    land(recv.at[1], later1)
-    place(e1, hy1[0], 0)
-    place(hx1.at[1], hc1[1, 0], 0)
-    place(hx1.at[0], hc1[0, 0], 0)
-    place(hx1.at[0], hc1[0, 1], 1)
-    first_s, first_t = pair1(0)
-    first_d = first_t - FAR * hx1[0]
-    xd1[0] = first_d
-    xs1[0] = hx1[0] - first_d
-    low = slice(PAD - 2, PAD)
-
-    lift1(low)
-    edge, _ = sums(e1[cx - 2, :, low], e1[cx - 1, :, low])
-    edge_d = hx1[1, :, low] - FAR * edge
-    xd1[hx, :, low] = edge_d
-    xs1[hx, :, low] = edge - edge_d
+        round2 += post(xl.at[:, rows_s, :], xlow.at[:, rows_d, :], 1, dy, 3)
+        round2 += post(xh.at[:, rows_s, :], xhigh.at[:, rows_d, :], -1, dy, 3)
+    round2 += post(e2.at[:, pl.ds(PAD, PAD), :], e2.at[:, y_high, :], 0, -1, 3)
+    round2 += post(e2.at[:, pl.ds(hy, PAD), :], e2.at[:, y_low, :], 0, 1, 3)
+
+    land(recv.at[2], later1)
+
+    def place(ref, rows, side):
+        if side == 0:
+            ref[..., PAD - 2 : PAD - 1, :] = rows
+            ref[..., PAD - 1 : PAD, :] = jnp.zeros_like(rows)
+        else:
+            ref[..., top : top + 1, :] = -ROOT3 * rows
+            ref[..., top + 1 : top + 2, :] = rows
+
+    for side in range(2):
+        place(e1, hy1[side], side)
+        for x in range(2):
+            place(hx1.at[x], hc1[x, side], side)
+    lift1(slice(PAD - 2, PAD))
+    lift1(slice(top, top + 2))
+    wide = slice(PAD - 2, top + 2)
+    _, edge = pair1(0, wide)
+    detail = edge - FAR * hx1[0, :, wide]
+    xd1[0, :, wide] = detail
+    xs1[0, :, wide] = hx1[0, :, wide] - detail
+    edge, _ = pair1(hx - 1, wide)
+    detail = hx1[1, :, wide] - FAR * edge
+    xd1[hx, :, wide] = detail
+    xs1[hx, :, wide] = edge - detail
 
     def cols1(src, det, smo):
         def step(n, carry):
@@ -277,38 +319,10 @@
 
         lax.fori_loop(0, hx + 1, step, 0)
 
-    rows1 = hy + PAD
-    parts1 = ((0, chunk), (chunk, hx + 1))
-
-    def depth1(ref):
-        magnitude = jnp.zeros((PAD, LANES), jnp.float32)
-        for lo, hi in parts1:
-            rows = lines(ref, slice(lo, hi), slice(0, rows1))
-            if ref is s1s:
-                ref[lo:hi, 1] = times(rows, w1.at[:, :, LANES : 2 * LANES]).reshape(
-                    hi - lo, rows1, LANES)
-                continue
-            got = times(rows, w1)
-            for h in range(2):
-                ref[lo:hi, h] = got[:, h * LANES : (h + 1) * LANES].reshape(hi - lo, rows1, LANES)
-            if ref is d1d:
-                inside = got[:, LANES:].reshape(hi - lo, rows1, LANES)[:chunk, :hy]
-                magnitude = magnitude + jnp.sum(
-                    jnp.abs(inside).reshape(chunk * hy // PAD, PAD, LANES), axis=0)
-        return magnitude
-
     cols1(xd1, d1d, d1s)
-    mine[...] = jnp.sum(depth1(d1d), axis=0, keepdims=True)
-    landed = 0
-    for k, d in enumerate(peers):
-        landed += post(mine, rows_in.at[k], d[0], d[1], 3)
-
     cols1(xs1, s1d, s1s)
-    depth1(d1s)
-    depth1(s1d)
-    depth1(s1s)
-
-    land(recv.at[2], round2)
+
+    land(recv.at[3], round2)
     every = slice(0, hy + 2 * PAD)
     before = xlow[0]
     xs2[0] = xlow[3]
@@ -353,7 +367,7 @@
     for i, band in enumerate(bands):
         b3[i] = times(band.reshape(n3 * h3, LANES), w3).reshape(n3, h3, LANES)
 
-    land(recv.at[3], landed)
+    land(recv.at[4], landed)
     acc = mine[...]
     for k in range(len(peers)):
         acc = acc + rows_in[k]
@@ -472,9 +486,8 @@
     n3, h3 = qx // 2 + 2, qy // 2 + PAD
     f32 = jnp.float32
     count = cx * nx * cy * ny * cz // 8
-    w1 = forward_matrix(cz)
     weights = [
-        halves(w1, cz), halves(w1[:, : cz // 2] @ forward_matrix(cz // 2), cz)[:, :, : cz // 2],
+        halves(forward_matrix(cz), cz), halves(forward_matrix(cz // 2), LANES),
         halves(forward_matrix(cz // 4), LANES), halves(inverse_matrix(cz), cz),
         halves(inverse_matrix(cz // 2), LANES), halves(inverse_matrix(cz // 4), LANES),
     ]
@@ -489,7 +502,7 @@
     )
     rows = 4 * cy + 4 * cx + 8 + 6 * (hy + 2 * PAD) + 2 * hx * PAD + nx * ny
     scratch = [
-        wide(cz, cz), wide(cz, LANES), wide(LANES, LANES),
+        wide(cz, cz), wide(LANES, LANES), wide(LANES, LANES),
         vmem(cx, 2, ey, LANES), vmem(2, 2, ey, LANES), vmem(2, 2, cy, LANES),
         vmem(2, cx, 2, 1, LANES), vmem(2, cx, 2, 1, LANES),
         vmem(2, 2, 2, 1, LANES), vmem(2, 2, 2, 1, LANES),
@@ -498,9 +511,9 @@
         vmem(4, ey2, LANES), vmem(2, ey2, LANES),
         vmem(qx + 2, ey2, LANES), vmem(qx + 4, ey2, LANES),
         vmem(n3, ey3, LANES), vmem(n3, ey3, LANES),
-        vmem(1, LANES), vmem(nx * ny - 1, 1, LANES), vmem(rows, 1, LANES),
-        pltpu.SemaphoreType.DMA((1,)), pltpu.SemaphoreType.DMA((4,)),
-        pltpu.SemaphoreType.DMA((2,)), pltpu.SemaphoreType.DMA((6,)),
+        vmem(1, LANES), vmem(nx * ny - 1, 1, LANES), vmem(max(rows, cz * cz // 32), 1, LANES),
+        pltpu.SemaphoreType.DMA((1,)), pltpu.SemaphoreType.DMA((5,)),
+        pltpu.SemaphoreType.DMA((2,)), pltpu.SemaphoreType.DMA((2,)),
     ]
     near = pl.BlockSpec(memory_space=pltpu.VMEM)
     passed = pl.pallas_call(

time: 21.9 us -> 21.1 us (0.963)
  Pallas kernels: 21.7 us -> 21 us
    pallas_call x1, Pallas kernels: 17.6 us -> 16.8 us  [on_device(): pl.pallas_call(functools.partial(kernel, (cx, cy, cz), nx, ny), out_shape...]
where the time goes in v3:
time: 21.1 us; the launch traced here: 21 us
  Pallas kernels  21 us (100%)
    pallas_call x1, Pallas kernels, on_device(): pl.pallas_call(functools.partial(kernel, (cx, cy, cz), nx, ny), out_shape...  16.8 us
    pallas_call x1, Pallas kernels, on_device(): pl.pallas_call(functools.partial(finish, (cx, cy, cz), count), out_shape=...  4.15 us

profile of v3, /device:TPU:0, one launch (start us, length us, event | category | flops | bytes accessed | tf_op | source)
XLA Modules:
  0.0 21.0 jit_solution(5091370184750416655)
XLA Ops:
  0.0 16.8 %shard_map.73 = (f32[17,2,40,128]{3,2,1,0:T(8,128)S(1)}, f32[17,2,40,128]{3,2,1,0:T(8,128)S(1)}, f32[17,2,40,128]{3,2,1,0:T(8,128)S(1)}, f32[17,2,40,128]{3,2,1,...) custom-call(f32[32,64,256]{2,1,0:T(8,128)} %vol.1, ...), custom_call_target="tpu_custom_call" | custom-call | tf_op jit(solution)/shard_map/pallas_call | solution.py:519
  16.8 4.1 %shard_map.74 = f32[32,64,256]{2,1,0:T(8,128)} custom-call(f32[17,2,40,128]{3,2,1,0:T(8,128)S(1)} %get-tuple-element.18.d1d, f32[17,2,40,128]{3,2,1,0:T(8,128)S(1)} %get-tuple-element.19.d1s, f32[17,2,40,128]{3,2,1,0:T(8,128)S(1)} %get-tuple-element.20.s1d, f32[17,2,40,128]{3,2,1,0:T(8,128)S(1)} %get-tuple-element.21.s1s, ...), custom_call_target="tpu_custom_call" | custom-call | tf_op jit(solution)/shard_map/pallas_call | solution.py:528

commit v4 on v3

--- a/solution.py
+++ b/solution.py
@@ -51,6 +51,19 @@
     return dot(high, w_ref[0]) + (dot(low, w_ref[0]) + dot(high, w_ref[1]))
 
 
+def folded(matrix):
+    high, low = halves(matrix, LANES)
+    return np.block([[high, low], [high, np.zeros_like(low)]])
+
+
+def times_folded(values, w_ref):
+    high = values.astype(jnp.bfloat16)
+    low = (values - high.astype(jnp.float32)).astype(jnp.bfloat16)
+    both = jnp.dot(jnp.concatenate([high, low], axis=1), w_ref[...],
+                   preferred_element_type=jnp.float32)
+    return both[:, :LANES] + both[:, LANES:]
+
+
 def shrink(values, noise):
     return values - jnp.clip(values, -noise, noise)
 
@@ -82,9 +95,26 @@
     return base * (1.0 / (HIGH * HIGH)), base * (1.0 / (HIGH * LOW)), base * (1.0 / (LOW * LOW))
 
 
-def kernel(shape, nx, ny, vol, g1, g2, g3, g4, g5, g6,
-           d1d, d1s, s1d, s1s, dd, ds, sd, ep3, b3, noise, v1, v2, v3,
-           w1, w2, w3,
+def spread(total, count_all):
+    return jnp.sum(total, axis=(0, 1), keepdims=True) * (
+        HIGH * HIGH * math.sqrt(math.pi / 2.0) / count_all)
+
+
+def inverse1(hx, one_x, put):
+    def step(n, carry):
+        d, before = carry
+        after, one = one_x(n + 1)
+        even, odd = undo(d, one, before)
+        put(2 * n, even)
+        put(2 * n + 1, odd)
+        return after, one
+
+    lax.fori_loop(0, hx, step, one_x(0), unroll=4)
+
+
+def kernel(shape, count_all, nx, ny, vol, g1, g2, g3, g4, g5, g6,
+           d1s, p1d, p1s1, dd, ds, sd, ep3, b3, noise, v1, v2, v3,
+           w1, w2, w3, d1d, s1d, s1s,
            e1, hx1, sx1, hy1, sy1, hc1, sc1, xd1, xs1,
            e2, xl, xh, xlow, xhigh, xd2, xs2, t3d, t3s,
            mine, rows_in, dummy, send, recv, lsem, wsem):
@@ -226,7 +256,7 @@
     land(wsem.at[1], sum(2 * math.prod(dst.shape) // (4 * LANES) for _, dst in more))
     done = hy - PAD
     rows = s1s[1:hx, 0, PAD : PAD + done].reshape((hx - 1) * done, LANES)
-    e2[0 : hx - 1, PAD : PAD + done] = times(rows, w2).reshape(hx - 1, done, LANES)
+    e2[0 : hx - 1, PAD : PAD + done] = times_folded(rows, w2).reshape(hx - 1, done, LANES)
 
     land(recv.at[0], noise1)
     edge = hy1[0, :, 1].reshape(hx, 2, 1, LANES)
@@ -255,7 +285,7 @@
     rows = jnp.concatenate(
         [s1s[1:hx, 0, PAD + done : PAD + hy].reshape((hx - 1) * PAD, LANES), s1s[hx, 0, own]],
         axis=0)
-    got = times(rows, w2)
+    got = times_folded(rows, w2)
     e2[0 : hx - 1, PAD + done : PAD + hy] = got[: (hx - 1) * PAD].reshape(hx - 1, PAD, LANES)
     e2[hx - 1, own] = got[(hx - 1) * PAD :]
 
@@ -321,6 +351,31 @@
 
     cols1(xd1, d1d, d1s)
     cols1(xs1, s1d, s1s)
+
+    land(recv.at[4], landed)
+    acc = mine[...]
+    for k in range(len(peers)):
+        acc = acc + rows_in[k]
+    noise[...] = acc
+    far1, mid1, near1 = limits(spread(acc, count_all), 1)
+
+    def put_into(dst, h):
+        def put(n, rows):
+            if h is None:
+                dst[n] = rows
+            else:
+                dst[n, h] = rows
+        return put
+
+    def bands1(det, smo, h, limit_d, limit_s):
+        def one_x(n):
+            d = shrink(det[n, h], limit_d)
+            return d, shrink(smo[n, h], limit_s) + d
+        return one_x
+
+    for h in range(2):
+        inverse1(hx, bands1(d1d, s1d, h, far1, mid1), put_into(p1d, h))
+    inverse1(hx, bands1(d1s, s1s, 1, mid1, near1), put_into(p1s1, None))
 
     land(recv.at[3], round2)
     every = slice(0, hy + 2 * PAD)
@@ -365,45 +420,18 @@
     for src in (t3d, t3s):
         bands += forward_rows(src[:, pl.ds(0, h3, stride=2), :], src[:, pl.ds(1, h3, stride=2), :])
     for i, band in enumerate(bands):
-        b3[i] = times(band.reshape(n3 * h3, LANES), w3).reshape(n3, h3, LANES)
-
-    land(recv.at[4], landed)
-    acc = mine[...]
-    for k in range(len(peers)):
-        acc = acc + rows_in[k]
-    noise[...] = acc
+        b3[i] = times_folded(band.reshape(n3 * h3, LANES), w3).reshape(n3, h3, LANES)
+
     land(send.at[0], sent[0])
 
 
-def finish(shape, count_all, d1d, d1s, s1d, s1s, dd, ds, sd, ep3, b3, total, v1, v2, v3, out,
-           ss, r2, r1, s0, p1d, p1s, o1, ob, osem):
+def finish(shape, count_all, d1s, p1d, p1s1, dd, ds, sd, ep3, b3, total, v1, v2, v3, out,
+           ss, r2, r1, s0, p1s0, o1, ob, osem):
     cx, cy, cz = shape
     hx, hy, qx, qy = cx // 2, cy // 2, cx // 4, cy // 4
     n3, h3, x2, yrows = qx // 2 + 2, qy // 2 + PAD, qx + 2, qy + 2 * PAD
-    noise = jnp.sum(total[...], axis=(0, 1), keepdims=True) * (
-        HIGH * HIGH * math.sqrt(math.pi / 2.0) / count_all)
-
-    far1, mid1, near1 = limits(noise, 1)
-
-    def inv1(det, smo, h, dst, limit_d, limit_s):
-        def one_x(n):
-            d = shrink(det[n, h], limit_d)
-            s = s0[n] if limit_s is None else shrink(smo[n, h], limit_s)
-            return d, s + d
-
-        def step(n, carry):
-            d, before = carry
-            after, one = one_x(n + 1)
-            even, odd = undo(d, one, before)
-            dst[2 * n, h] = even
-            dst[2 * n + 1, h] = odd
-            return after, one
-
-        lax.fori_loop(0, hx, step, one_x(0), unroll=4)
-
-    for h in range(2):
-        inv1(d1d, s1d, h, p1d, far1, mid1)
-    inv1(d1s, s1s, 1, p1s, mid1, near1)
+    noise = spread(total[...], count_all)
+
 
     far3, mid3, near3 = (v.reshape(1, 1, 1) for v in limits(noise, 3))
     lane3 = lax.broadcasted_iota(jnp.int32, (n3, h3, LANES), 2)
@@ -421,7 +449,7 @@
     even, odd = undo(y_d, one, pltpu.roll(one, 1, 1))
     r2[:, pl.ds(0, h3, stride=2), :] = even
     r2[:, pl.ds(1, h3, stride=2), :] = odd
-    back = times(r2[...].reshape(x2 * yrows, LANES), v3).reshape(x2, yrows, LANES)
+    back = times_folded(r2[...].reshape(x2 * yrows, LANES), v3).reshape(x2, yrows, LANES)
 
     far2, mid2, near2 = limits(noise, 2)
     lane2 = lax.broadcasted_iota(jnp.int32, (x2, yrows, LANES), 2)
@@ -448,16 +476,26 @@
 
     lax.fori_loop(0, qx + 1, inv2, one_x(0), unroll=3)
     x1, y1 = hx + 2, hy + PAD
-    back = times(r1[:, PAD : PAD + y1].reshape(x1 * y1, LANES), v2).reshape(x1, y1, LANES)
+    back = times_folded(r1[:, PAD : PAD + y1].reshape(x1 * y1, LANES), v2).reshape(x1, y1, LANES)
     s0[...] = back[1:]
-    inv1(d1s, s1s, 0, p1s, mid1, None)
+    _, mid1, _ = limits(noise, 1)
+
+    def low_x(n):
+        d = shrink(d1s[n, 0], mid1)
+        return d, s0[n] + d
+
+    def put_low(n, rows):
+        p1s0[n] = rows
+
+    inverse1(hx, low_x, put_low)
 
     def inv1_y(n):
         for h in range(2):
             y_d = p1d[n, h, 0:hy]
             y_n = p1d[n, h, 1 : hy + 1]
-            s = p1s[n, h, PAD : PAD + hy]
-            s_b = p1s[n, h, PAD - 1 : PAD - 1 + hy]
+            p1s = p1s1 if h else p1s0
+            s = p1s[n, PAD : PAD + hy]
+            s_b = p1s[n, PAD - 1 : PAD - 1 + hy]
             even, odd = undo(y_d, s + y_n, s_b + y_d)
             o1[n, h, pl.ds(0, hy, stride=2), :] = even
             o1[n, h, pl.ds(1, hy, stride=2), :] = odd
@@ -487,22 +525,24 @@
     f32 = jnp.float32
     count = cx * nx * cy * ny * cz // 8
     weights = [
-        halves(forward_matrix(cz), cz), halves(forward_matrix(cz // 2), LANES),
-        halves(forward_matrix(cz // 4), LANES), halves(inverse_matrix(cz), cz),
-        halves(inverse_matrix(cz // 2), LANES), halves(inverse_matrix(cz // 4), LANES),
+        halves(forward_matrix(cz), cz), folded(forward_matrix(cz // 2)),
+        folded(forward_matrix(cz // 4)), halves(inverse_matrix(cz), cz),
+        folded(inverse_matrix(cz // 2)), folded(inverse_matrix(cz // 4)),
     ]
     vmem = lambda *s: pltpu.VMEM(s, f32)
     ey, ey2, ey3 = cy + 2 * PAD, hy + 2 * PAD, qy + 2 * PAD
-    wide = lambda *s: pltpu.VMEM((2,) + s, jnp.bfloat16)
+    wide = lambda *s: pltpu.VMEM(s, jnp.bfloat16)
+    pair = (2 * LANES, 2 * LANES)
     made = (
-        *[vmem(hx + 1, 2, hy + PAD, LANES) for _ in range(4)],
-        *[vmem(qx + 2, ey3, LANES) for _ in range(3)],
+        vmem(hx + 1, 2, hy + PAD, LANES), vmem(cx, 2, hy + PAD, LANES),
+        vmem(cx, hy + PAD, LANES), *[vmem(qx + 2, ey3, LANES) for _ in range(3)],
         vmem(qx + 4, ey3, LANES), vmem(4, n3, h3, LANES), vmem(1, LANES),
-        wide(cz, cz), wide(LANES, LANES), wide(LANES, LANES),
+        wide(2, cz, cz), wide(*pair), wide(*pair),
     )
     rows = 4 * cy + 4 * cx + 8 + 6 * (hy + 2 * PAD) + 2 * hx * PAD + nx * ny
     scratch = [
-        wide(cz, cz), wide(LANES, LANES), wide(LANES, LANES),
+        wide(2, cz, cz), wide(*pair), wide(*pair),
+        *[vmem(hx + 1, 2, hy + PAD, LANES) for _ in range(3)],
         vmem(cx, 2, ey, LANES), vmem(2, 2, ey, LANES), vmem(2, 2, cy, LANES),
         vmem(2, cx, 2, 1, LANES), vmem(2, cx, 2, 1, LANES),
         vmem(2, 2, 2, 1, LANES), vmem(2, 2, 2, 1, LANES),
@@ -517,7 +557,7 @@
     ]
     near = pl.BlockSpec(memory_space=pltpu.VMEM)
     passed = pl.pallas_call(
-        functools.partial(kernel, (cx, cy, cz), nx, ny),
+        functools.partial(kernel, (cx, cy, cz), count, nx, ny),
         out_shape=made,
         in_specs=[pl.BlockSpec(memory_space=pltpu.HBM)] * 7,
         out_specs=(near,) * len(made),
@@ -533,8 +573,7 @@
         scratch_shapes=[
             vmem(qx + 2, ey3, LANES), vmem(qx + 2, ey3, LANES), vmem(hx + 2, 2 * ey3, LANES),
             vmem(hx + 1, hy + PAD, LANES),
-            vmem(cx, 2, hy + PAD, LANES), vmem(cx, 2, hy + PAD, LANES),
-            vmem(cx, 2, cy, LANES), vmem(cx, cy, cz), pltpu.SemaphoreType.DMA((cx // 8,)),
+            vmem(cx, hy + PAD, LANES), vmem(cx, 2, cy, LANES), vmem(cx, cy, cz), pltpu.SemaphoreType.DMA((cx // 8,)),
         ],
         compiler_params=pltpu.CompilerParams(vmem_limit_bytes=24 * 1024 * 1024),
     )(*passed)

time: 21.1 us -> 20.2 us (0.957)
  Pallas kernels: 21 us -> 20 us
    pallas_call x1, Pallas kernels: 4.15 us -> 3.35 us  [on_device(): pl.pallas_call(functools.partial(finish, (cx, cy, cz), count), out_shape=...]
where the time goes in v4:
time: 20.2 us; the launch traced here: 20 us
  Pallas kernels  20 us (99%)
    pallas_call x1, Pallas kernels, on_device(): pl.pallas_call(functools.partial(kernel, (cx, cy, cz), count, nx, ny), ou...  16.7 us
    pallas_call x1, Pallas kernels, on_device(): pl.pallas_call(functools.partial(finish, (cx, cy, cz), count), out_shape=...  3.35 us

profile of v4, /device:TPU:0, one launch (start us, length us, event | category | flops | bytes accessed | tf_op | source)
XLA Modules:
  0.0 20.0 jit_solution(801359182742093486)
XLA Ops:
  0.0 16.7 %shard_map.73 = (f32[17,2,40,128]{3,2,1,0:T(8,128)S(1)}, f32[32,2,40,128]{3,2,1,0:T(8,128)S(1)}, f32[32,40,128]{2,1,0:T(8,128)S(1)}, f32[10,32,128]{2,1,0:T(8,12...) custom-call(f32[32,64,256]{2,1,0:T(8,128)} %vol.1, ...), custom_call_target="tpu_custom_call" | custom-call | tf_op jit(solution)/shard_map/pallas_call | solution.py:559
  16.7 3.3 %shard_map.74 = f32[32,64,256]{2,1,0:T(8,128)} custom-call(f32[17,2,40,128]{3,2,1,0:T(8,128)S(1)} %get-tuple-element.17.d1s, f32[32,2,40,128]{3,2,1,0:T(8,128)S(1)} %get-tuple-element.18.p1d, f32[32,40,128]{2,1,0:T(8,128)S(1)} %get-tuple-element.19.p1s1, f32[10,32,128]{2,1,0:T(8,128)S(1)} %get-tuple-element.20.dd, f32[10,32,128]{2,1,0:T(8,128)S(1)} %get-tuple-element.21.ds, ...), custom_call_target="tpu_custom_call" | custom-call | tf_op jit(solution)/shard_map/pallas_call | solution.py:568

commit v5 on v4

--- a/solution.py
+++ b/solution.py
@@ -115,7 +115,7 @@
 def kernel(shape, count_all, nx, ny, vol, g1, g2, g3, g4, g5, g6,
            d1s, p1d, p1s1, dd, ds, sd, ep3, b3, noise, v1, v2, v3,
            w1, w2, w3, d1d, s1d, s1s,
-           e1, hx1, sx1, hy1, sy1, hc1, sc1, xd1, xs1,
+           e1, lx, rx, hx1, sx1, hy1, sy1, hc1, sc1, xd1, xs1,
            e2, xl, xh, xlow, xhigh, xd2, xs2, t3d, t3s,
            mine, rows_in, dummy, send, recv, lsem, wsem):
     cx, cy, cz = shape
@@ -198,6 +198,13 @@
     for x in range(2):
         sc1[x, 1] = sums(sx1[x, :, 0:1], sx1[x, :, 1:2])[1]
         sc1[x, 0] = sums(sx1[x, :, cy - 2 : cy - 1], sx1[x, :, cy - 1 : cy])[0]
+    line = lax.broadcasted_iota(jnp.int32, (hy, LANES), 0)
+    for x in range(2):
+        load = lambda start: sx1[x, 1 - x, pl.ds(start, hy, stride=2), :]
+        smooth, part = sums(load(0), load(1))
+        detail = part - jnp.where(line > 0, FAR * pltpu.roll(smooth, 1, 0), 0.0)
+        lx[x, 0] = detail
+        lx[x, 1] = smooth - jnp.where(line < hy - 1, pltpu.roll(detail, hy - 1, 0), 0.0)
     pl.semaphore_wait(barrier, len(peers))
     step = (1, -1)
     post_x = lambda x, h, g: post(
@@ -205,9 +212,13 @@
     post_y = lambda y, h, g: post(sy1.at[y, :, h], hy1.at[y, :, h], 0, step[y], g)
     post_c = lambda x, y, h, g: post(
         sc1.at[x, y, h], hc1.at[x, y, h], step[x], step[y], g)
-    noise1 = post_c(0, 0, 1, 0) + post_x(0, 1, 0) + post_y(0, 1, 0)
-    coarse1 = post_c(1, 1, 0, 1) + post_x(1, 0, 1) + post_y(1, 0, 1)
+    post_l = lambda x, k, g: post(lx.at[x, k], rx.at[x, k], step[x], 0, g)
+    noise1 = post_c(0, 0, 1, 0)
+    coarse1 = post_c(1, 1, 0, 1) + post_l(1, 1, 1)
+    noise1 += post_l(0, 0, 0) + post_y(0, 1, 0)
+    coarse1 += post_y(1, 0, 1)
     later1 = (post_c(0, 0, 0, 2) + post_c(1, 1, 1, 2) + post_x(0, 0, 2) + post_x(1, 1, 2)
+              + post_l(0, 1, 2) + post_l(1, 0, 2)
               + post_y(0, 0, 2) + post_y(1, 1, 2))
     for h in range(2):
         later1 += post_c(0, 1, h, 2) + post_c(1, 0, h, 2)
@@ -240,16 +251,16 @@
         load = lambda start: xd1[n, 1, pl.ds(start, hy, stride=2), :]
         _, t0 = sums(load(PAD), load(PAD + 1))
         sm, _ = sums(load(PAD - 2), load(PAD - 1))
-        return jnp.abs(t0 - FAR * sm)
+        return t0 - FAR * sm
 
     def fold(values):
         return jnp.sum(values.reshape(hy // PAD, PAD, LANES), axis=0)
 
-    known = lax.broadcasted_iota(jnp.int32, (hy, LANES), 0) > 0
+    known = line > 0
 
     def inside(n, magnitude):
         shrunk(n)
-        return magnitude + fold(jnp.where(known, finest(n), 0.0))
+        return magnitude + fold(jnp.where(known, jnp.abs(finest(n)), 0.0))
 
     lift1(own1)
     magnitude = lax.fori_loop(1, hx, inside, jnp.zeros((PAD, LANES), jnp.float32))
@@ -262,25 +273,27 @@
     edge = hy1[0, :, 1].reshape(hx, 2, 1, LANES)
     edge_s, edge_t = sums(edge[:, 0], edge[:, 1])
     edge_d = edge_t - FAR * jnp.concatenate([hc1[0, 0, 1][None], edge_s[:-1]], axis=0)
-    xd1[0, 1, own1] = sums(e1[0, 1, own1], e1[1, 1, own1])[1] - FAR * hx1[0, 1, own1]
+    xd1[0, 1, own1] = sums(e1[0, 1, own1], e1[1, 1, own1])[1]
     xd1[0, 1, PAD - 2 : PAD - 1] = edge_d[0]
     xd1[0, 1, PAD - 1 : PAD] = jnp.zeros((1, LANES), jnp.float32)
     _, edge_t = sums(xd1[1:hx, 1, PAD : PAD + 1], xd1[1:hx, 1, PAD + 1 : PAD + 2])
     row = jnp.sum(jnp.abs(edge_t - FAR * edge_d[1:]), axis=0)
-    mine[...] = row + jnp.sum(magnitude + fold(finest(0)), axis=0, keepdims=True)
+    mine[...] = row + jnp.sum(magnitude + fold(jnp.abs(finest(0) - FAR * rx[0, 0])), axis=0, keepdims=True)
     landed = 0
     for k, d in enumerate(peers):
         landed += post(mine, rows_in.at[k], d[0], d[1], 4)
 
     land(recv.at[1], coarse1)
     edge, _ = sums(e1[cx - 2, 0, own1], e1[cx - 1, 0, own1])
-    xs1[hx, 0, own1] = edge - (hx1[1, 0, own1] - FAR * edge)
+    xs1[hx, 0, own1] = edge * (1.0 + FAR)
     shrunk(hx)
+    s1s[hx, 0, own] = s1s[hx, 0, own] - rx[1, 1]
     edge = hy1[1, :, 0].reshape(hx, 2, 1, LANES)
     edge_s, edge_t = sums(edge[:, 0], edge[:, 1])
     after = jnp.concatenate([edge_t[1:], hc1[1, 1, 0][None]], axis=0)
     last_t = edge_s - (after - FAR * edge_s)
     last_s, _ = sums(xs1[1 : hx + 1, 0, top - 2 : top - 1], xs1[1 : hx + 1, 0, top - 1 : top])
+    last_s = jnp.concatenate([last_s[:-1], last_s[-1:] - rx[1, 1, hy - 1 : hy][None]], axis=0)
     s1s[1 : hx + 1, 0, PAD + hy - 1 : PAD + hy] = last_s - (last_t - FAR * last_s)
     rows = jnp.concatenate(
         [s1s[1:hx, 0, PAD + done : PAD + hy].reshape((hx - 1) * PAD, LANES), s1s[hx, 0, own]],
@@ -304,7 +317,7 @@
     y_own, y_low, y_high = pl.ds(PAD, hy), pl.ds(0, PAD), pl.ds(PAD + hy, PAD)
     s_own, s_first, s_last = pl.ds(0, hy), pl.ds(0, PAD), pl.ds(hy - PAD, PAD)
     round2 = 0
-    for rows_s, rows_d, dy in ((s_last, y_low, 1), (s_first, y_high, -1), (s_own, y_own, 0)):
+    for rows_s, rows_d, dy in ((s_own, y_own, 0), (s_last, y_low, 1), (s_first, y_high, -1)):
         round2 += post(xl.at[:, rows_s, :], xlow.at[:, rows_d, :], 1, dy, 3)
         round2 += post(xh.at[:, rows_s, :], xhigh.at[:, rows_d, :], -1, dy, 3)
     round2 += post(e2.at[:, pl.ds(PAD, PAD), :], e2.at[:, y_high, :], 0, -1, 3)
@@ -320,6 +333,13 @@
             ref[..., top : top + 1, :] = -ROOT3 * rows
             ref[..., top + 1 : top + 2, :] = rows
 
+    for x in range(2):
+        detail, smooth = rx[x, 0], rx[x, 1]
+        smooth = smooth + jnp.where(line < hy - 1, pltpu.roll(detail, hy - 1, 0), 0.0)
+        part = detail + jnp.where(line > 0, FAR * pltpu.roll(smooth, 1, 0), 0.0)
+        odd = part + NEAR * smooth
+        hx1[x, 1 - x, pl.ds(PAD, hy, stride=2), :] = smooth - ROOT3 * odd
+        hx1[x, 1 - x, pl.ds(PAD + 1, hy, stride=2), :] = odd
     for side in range(2):
         place(e1, hy1[side], side)
         for x in range(2):
@@ -356,8 +376,9 @@
     acc = mine[...]
     for k in range(len(peers)):
         acc = acc + rows_in[k]
-    noise[...] = acc
-    far1, mid1, near1 = limits(spread(acc, count_all), 1)
+    level = spread(acc, count_all)
+    noise[...] = jnp.broadcast_to(level, (PAD, LANES))
+    far1, mid1, near1 = limits(level, 1)
 
     def put_into(dst, h):
         def put(n, rows):
@@ -425,15 +446,15 @@
     land(send.at[0], sent[0])
 
 
-def finish(shape, count_all, d1s, p1d, p1s1, dd, ds, sd, ep3, b3, total, v1, v2, v3, out,
+def finish(shape, d1s, p1d, p1s1, dd, ds, sd, ep3, b3, total, v1, v2, v3, out,
            ss, r2, r1, s0, p1s0, o1, ob, osem):
     cx, cy, cz = shape
     hx, hy, qx, qy = cx // 2, cy // 2, cx // 4, cy // 4
     n3, h3, x2, yrows = qx // 2 + 2, qy // 2 + PAD, qx + 2, qy + 2 * PAD
-    noise = spread(total[...], count_all)
-
-
-    far3, mid3, near3 = (v.reshape(1, 1, 1) for v in limits(noise, 3))
+    noise = total[0:1]
+
+
+    far3, mid3, near3 = (v[None] for v in limits(noise, 3))
     lane3 = lax.broadcasted_iota(jnp.int32, (n3, h3, LANES), 2)
     b_dd, b_ds, b_sd = shrink(b3[0], far3), shrink(b3[1], mid3), shrink(b3[2], mid3)
     b_ss = jnp.where(lane3 < cz // 8, b3[3], shrink(b3[3], near3))
@@ -453,7 +474,7 @@
 
     far2, mid2, near2 = limits(noise, 2)
     lane2 = lax.broadcasted_iota(jnp.int32, (x2, yrows, LANES), 2)
-    ss[...] = jnp.where(lane2 < cz // 4, back, shrink(ep3[1 : qx + 3], near2.reshape(1, 1, 1)))
+    ss[...] = jnp.where(lane2 < cz // 4, back, shrink(ep3[1 : qx + 3], near2[None]))
 
     def one_x(n):
         d_d = shrink(dd[n], far2)
@@ -536,14 +557,15 @@
     made = (
         vmem(hx + 1, 2, hy + PAD, LANES), vmem(cx, 2, hy + PAD, LANES),
         vmem(cx, hy + PAD, LANES), *[vmem(qx + 2, ey3, LANES) for _ in range(3)],
-        vmem(qx + 4, ey3, LANES), vmem(4, n3, h3, LANES), vmem(1, LANES),
+        vmem(qx + 4, ey3, LANES), vmem(4, n3, h3, LANES), vmem(PAD, LANES),
         wide(2, cz, cz), wide(*pair), wide(*pair),
     )
     rows = 4 * cy + 4 * cx + 8 + 6 * (hy + 2 * PAD) + 2 * hx * PAD + nx * ny
     scratch = [
         wide(2, cz, cz), wide(*pair), wide(*pair),
         *[vmem(hx + 1, 2, hy + PAD, LANES) for _ in range(3)],
-        vmem(cx, 2, ey, LANES), vmem(2, 2, ey, LANES), vmem(2, 2, cy, LANES),
+        vmem(cx, 2, ey, LANES), vmem(2, 2, hy, LANES), vmem(2, 2, hy, LANES),
+        vmem(2, 2, ey, LANES), vmem(2, 2, cy, LANES),
         vmem(2, cx, 2, 1, LANES), vmem(2, cx, 2, 1, LANES),
         vmem(2, 2, 2, 1, LANES), vmem(2, 2, 2, 1, LANES),
         vmem(hx + 1, 2, ey, LANES), vmem(hx + 1, 2, ey, LANES),
@@ -566,7 +588,7 @@
             collective_id=0, has_side_effects=True, vmem_limit_bytes=56 * 1024 * 1024),
     )(volume, *[jnp.asarray(w) for w in weights])
     return pl.pallas_call(
-        functools.partial(finish, (cx, cy, cz), count),
+        functools.partial(finish, (cx, cy, cz)),
         out_shape=jax.ShapeDtypeStruct(volume.shape, f32),
         in_specs=[near] * len(made),
         out_specs=pl.BlockSpec(memory_space=pltpu.HBM),

time: 20.2 us -> 19.2 us (0.950)
  Pallas kernels: 20 us -> 19.1 us
    pallas_call x1, Pallas kernels: 16.7 us -> 15.8 us  [on_device(): pl.pallas_call(functools.partial(kernel, (cx, cy, cz), count, nx, ny), ou...]
where the time goes in v5:
time: 19.2 us; the launch traced here: 19.1 us
  Pallas kernels  19.1 us (99%)
    pallas_call x1, Pallas kernels, on_device(): pl.pallas_call(functools.partial(kernel, (cx, cy, cz), count, nx, ny), ou...  15.8 us
    pallas_call x1, Pallas kernels, on_device(): pl.pallas_call(functools.partial(finish, (cx, cy, cz)), out_shape=jax.Sha...  3.21 us

profile of v5, /device:TPU:0, one launch (start us, length us, event | category | flops | bytes accessed | tf_op | source)
XLA Modules:
  0.0 19.1 jit_solution(4377560740355441413)
XLA Ops:
  0.0 15.8 %shard_map.73 = (f32[17,2,40,128]{3,2,1,0:T(8,128)S(1)}, f32[32,2,40,128]{3,2,1,0:T(8,128)S(1)}, f32[32,40,128]{2,1,0:T(8,128)S(1)}, f32[10,32,128]{2,1,0:T(8,12...) custom-call(f32[32,64,256]{2,1,0:T(8,128)} %vol.1, ...), custom_call_target="tpu_custom_call" | custom-call | tf_op jit(solution)/shard_map/pallas_call | solution.py:581
  15.9 3.2 %shard_map.74 = f32[32,64,256]{2,1,0:T(8,128)} custom-call(f32[17,2,40,128]{3,2,1,0:T(8,128)S(1)} %get-tuple-element.17.d1s, f32[32,2,40,128]{3,2,1,0:T(8,128)S(1)} %get-tuple-element.18.p1d, f32[32,40,128]{2,1,0:T(8,128)S(1)} %get-tuple-element.19.p1s1, f32[10,32,128]{2,1,0:T(8,128)S(1)} %get-tuple-element.20.dd, f32[10,32,128]{2,1,0:T(8,128)S(1)} %get-tuple-element.21.ds, ...), custom_call_target="tpu_custom_call" | custom-call | tf_op jit(solution)/shard_map/pallas_call | solution.py:590

commit v6 on v5

--- a/solution.py
+++ b/solution.py
@@ -115,7 +115,7 @@
 def kernel(shape, count_all, nx, ny, vol, g1, g2, g3, g4, g5, g6,
            d1s, p1d, p1s1, dd, ds, sd, ep3, b3, noise, v1, v2, v3,
            w1, w2, w3, d1d, s1d, s1s,
-           e1, lx, rx, hx1, sx1, hy1, sy1, hc1, sc1, xd1, xs1,
+           e1, lx, rx, tc, fix, hx1, sx1, hy1, sy1, hc1, sc1, xd1, xs1,
            e2, xl, xh, xlow, xhigh, xd2, xs2, t3d, t3s,
            mine, rows_in, dummy, send, recv, lsem, wsem):
     cx, cy, cz = shape
@@ -168,6 +168,7 @@
 
     ep3[:, 0 : PAD // 2] = jnp.zeros((qx + 4, PAD // 2, LANES), jnp.float32)
     ep3[:, PAD // 2 + hy // 2 + PAD :] = jnp.zeros((qx + 4, PAD // 2, LANES), jnp.float32)
+    fix[...] = jnp.zeros((2, hy + 2 * PAD, LANES), jnp.float32)
     for ref in (dd, ds, sd):
         ref[:, 0 : PAD // 2] = jnp.zeros((qx + 2, PAD // 2, LANES), jnp.float32)
         ref[:, PAD // 2 + hy // 2 + PAD :] = jnp.zeros((qx + 2, PAD // 2, LANES), jnp.float32)
@@ -214,10 +215,11 @@
         sc1.at[x, y, h], hc1.at[x, y, h], step[x], step[y], g)
     post_l = lambda x, k, g: post(lx.at[x, k], rx.at[x, k], step[x], 0, g)
     noise1 = post_c(0, 0, 1, 0)
-    coarse1 = post_c(1, 1, 0, 1) + post_l(1, 1, 1)
+    coarse1 = post_l(1, 1, 1)
     noise1 += post_l(0, 0, 0) + post_y(0, 1, 0)
     coarse1 += post_y(1, 0, 1)
-    later1 = (post_c(0, 0, 0, 2) + post_c(1, 1, 1, 2) + post_x(0, 0, 2) + post_x(1, 1, 2)
+    later1 = (post_c(1, 1, 0, 2) + post(sc1.at[1, 1, 0], tc.at[0], 0, -1, 2)
+              + post(sc1.at[1, 1, 0], tc.at[1], -1, 0, 2) + post_c(0, 0, 0, 2) + post_c(1, 1, 1, 2) + post_x(0, 0, 2) + post_x(1, 1, 2)
               + post_l(0, 1, 2) + post_l(1, 0, 2)
               + post_y(0, 0, 2) + post_y(1, 1, 2))
     for h in range(2):
@@ -290,7 +292,7 @@
     s1s[hx, 0, own] = s1s[hx, 0, own] - rx[1, 1]
     edge = hy1[1, :, 0].reshape(hx, 2, 1, LANES)
     edge_s, edge_t = sums(edge[:, 0], edge[:, 1])
-    after = jnp.concatenate([edge_t[1:], hc1[1, 1, 0][None]], axis=0)
+    after = jnp.concatenate([edge_t[1:], jnp.zeros_like(edge_t[:1])], axis=0)
     last_t = edge_s - (after - FAR * edge_s)
     last_s, _ = sums(xs1[1 : hx + 1, 0, top - 2 : top - 1], xs1[1 : hx + 1, 0, top - 1 : top])
     last_s = jnp.concatenate([last_s[:-1], last_s[-1:] - rx[1, 1, hy - 1 : hy][None]], axis=0)
@@ -333,6 +335,12 @@
             ref[..., top : top + 1, :] = -ROOT3 * rows
             ref[..., top + 1 : top + 2, :] = rows
 
+    corners = jnp.concatenate(
+        [sc1[1, 1, 0], tc[0], tc[1], hc1[1, 1, 0], jnp.zeros((PAD - 4, LANES), jnp.float32)], axis=0)
+    corners = times_folded(corners, w2)
+    for i in range(4):
+        at = PAD - 1 + hy * (i % 2)
+        fix[i // 2, at : at + 1] = corners[i : i + 1]
     for x in range(2):
         detail, smooth = rx[x, 0], rx[x, 1]
         smooth = smooth + jnp.where(line < hy - 1, pltpu.roll(detail, hy - 1, 0), 0.0)
@@ -406,7 +414,9 @@
         if m == qx:
             smooth, part = None, xhigh[0]
         elif m == -1:
-            smooth, part = sums(xlow[1], xlow[2])
+            smooth, part = sums(xlow[1], xlow[2] + fix[0])
+        elif m == qx - 1:
+            smooth, part = sums(e2[hx - 2, every], e2[hx - 1, every] + fix[1])
         else:
             smooth, part = pair2(m, every)
         detail = part - FAR * before
@@ -495,7 +505,7 @@
             r1[2 * n + i, pl.ds(1, yrows, stride=2), :] = odd
         return after
 
-    lax.fori_loop(0, qx + 1, inv2, one_x(0), unroll=3)
+    lax.fori_loop(0, qx + 1, inv2, one_x(0), unroll=True)
     x1, y1 = hx + 2, hy + PAD
     back = times_folded(r1[:, PAD : PAD + y1].reshape(x1 * y1, LANES), v2).reshape(x1, y1, LANES)
     s0[...] = back[1:]
@@ -521,7 +531,7 @@
             o1[n, h, pl.ds(0, hy, stride=2), :] = even
             o1[n, h, pl.ds(1, hy, stride=2), :] = odd
 
-    layers = 8
+    layers = 4
     outs = []
     for n in range(layers):
         inv1_y(n)
@@ -560,11 +570,12 @@
         vmem(qx + 4, ey3, LANES), vmem(4, n3, h3, LANES), vmem(PAD, LANES),
         wide(2, cz, cz), wide(*pair), wide(*pair),
     )
-    rows = 4 * cy + 4 * cx + 8 + 6 * (hy + 2 * PAD) + 2 * hx * PAD + nx * ny
+    rows = 4 * cy + 4 * cx + 10 + 6 * (hy + 2 * PAD) + 2 * hx * PAD + nx * ny
     scratch = [
         wide(2, cz, cz), wide(*pair), wide(*pair),
         *[vmem(hx + 1, 2, hy + PAD, LANES) for _ in range(3)],
         vmem(cx, 2, ey, LANES), vmem(2, 2, hy, LANES), vmem(2, 2, hy, LANES),
+        vmem(2, 1, LANES), vmem(2, ey2, LANES),
         vmem(2, 2, ey, LANES), vmem(2, 2, cy, LANES),
         vmem(2, cx, 2, 1, LANES), vmem(2, cx, 2, 1, LANES),
         vmem(2, 2, 2, 1, LANES), vmem(2, 2, 2, 1, LANES),
@@ -595,7 +606,7 @@
         scratch_shapes=[
             vmem(qx + 2, ey3, LANES), vmem(qx + 2, ey3, LANES), vmem(hx + 2, 2 * ey3, LANES),
             vmem(hx + 1, hy + PAD, LANES),
-            vmem(cx, hy + PAD, LANES), vmem(cx, 2, cy, LANES), vmem(cx, cy, cz), pltpu.SemaphoreType.DMA((cx // 8,)),
+            vmem(cx, hy + PAD, LANES), vmem(cx, 2, cy, LANES), vmem(cx, cy, cz), pltpu.SemaphoreType.DMA((cx // 4,)),
         ],
         compiler_params=pltpu.CompilerParams(vmem_limit_bytes=24 * 1024 * 1024),
     )(*passed)

time: 19.2 us -> 18.6 us (0.969)
  Pallas kernels: 19.1 us -> 18.4 us
    pallas_call x1, Pallas kernels: 3.21 us -> 2.8 us  [on_device(): pl.pallas_call(functools.partial(finish, (cx, cy, cz)), out_shape=jax.Sha...]
    pallas_call x1, Pallas kernels: 15.8 us -> 15.6 us  [on_device(): pl.pallas_call(functools.partial(kernel, (cx, cy, cz), count, nx, ny), ou...]
where the time goes in v6:
time: 18.6 us; the launch traced here: 18.4 us
  Pallas kernels  18.4 us (99%)
    pallas_call x1, Pallas kernels, on_device(): pl.pallas_call(functools.partial(kernel, (cx, cy, cz), count, nx, ny), ou...  15.6 us
    pallas_call x1, Pallas kernels, on_device(): pl.pallas_call(functools.partial(finish, (cx, cy, cz)), out_shape=jax.Sha...  2.8 us

profile of v6, /device:TPU:0, one launch (start us, length us, event | category | flops | bytes accessed | tf_op | source)
XLA Modules:
  0.0 18.4 jit_solution(2030127182862764472)
XLA Ops:
  0.0 15.6 %shard_map.73 = (f32[17,2,40,128]{3,2,1,0:T(8,128)S(1)}, f32[32,2,40,128]{3,2,1,0:T(8,128)S(1)}, f32[32,40,128]{2,1,0:T(8,128)S(1)}, f32[10,32,128]{2,1,0:T(8,12...) custom-call(f32[32,64,256]{2,1,0:T(8,128)} %vol.1, ...), custom_call_target="tpu_custom_call" | custom-call | tf_op jit(solution)/shard_map/pallas_call | solution.py:592
  15.6 2.8 %shard_map.74 = f32[32,64,256]{2,1,0:T(8,128)} custom-call(f32[17,2,40,128]{3,2,1,0:T(8,128)S(1)} %get-tuple-element.17.d1s, f32[32,2,40,128]{3,2,1,0:T(8,128)S(1)} %get-tuple-element.18.p1d, f32[32,40,128]{2,1,0:T(8,128)S(1)} %get-tuple-element.19.p1s1, f32[10,32,128]{2,1,0:T(8,128)S(1)} %get-tuple-element.20.dd, f32[10,32,128]{2,1,0:T(8,128)S(1)} %get-tuple-element.21.ds, ...), custom_call_target="tpu_custom_call" | custom-call | tf_op jit(solution)/shard_map/pallas_call | solution.py:601

commit v7 on v6

--- a/solution.py
+++ b/solution.py
@@ -62,6 +62,20 @@
     both = jnp.dot(jnp.concatenate([high, low], axis=1), w_ref[...],
                    preferred_element_type=jnp.float32)
     return both[:, :LANES] + both[:, LANES:]
+
+
+def half_product(matrix, h):
+    high, low = halves(matrix, len(matrix))
+    mine = slice(h * LANES, (h + 1) * LANES)
+    return np.concatenate([high[mine], high[mine], low[mine]], axis=0)
+
+
+def times_half(values, w_ref):
+    high = values.astype(jnp.bfloat16)
+    low = (values - high.astype(jnp.float32)).astype(jnp.bfloat16)
+    dot = functools.partial(jnp.dot, preferred_element_type=jnp.float32)
+    return (dot(jnp.concatenate([high, low], axis=1), w_ref[: 2 * LANES])
+            + dot(high, w_ref[2 * LANES :]))
 
 
 def shrink(values, noise):
@@ -112,9 +126,17 @@
     lax.fori_loop(0, hx, step, one_x(0), unroll=4)
 
 
-def kernel(shape, count_all, nx, ny, vol, g1, g2, g3, g4, g5, g6,
-           d1s, p1d, p1s1, dd, ds, sd, ep3, b3, noise, v1, v2, v3,
-           w1, w2, w3, d1d, s1d, s1s,
+def inverse1_y(hy, det, smo, n, dst):
+    y_d, y_n = det[n, 0:hy], det[n, 1 : hy + 1]
+    even, odd = undo(
+        y_d, smo[n, PAD : PAD + hy] + y_n, smo[n, PAD - 1 : PAD - 1 + hy] + y_d)
+    dst[n, pl.ds(0, hy, stride=2), :] = even
+    dst[n, pl.ds(1, hy, stride=2), :] = odd
+
+
+def kernel(shape, count_all, nx, ny, vol, g1, g2, g3, g4, g5, g6, g7,
+           d1s, p1d0, known1, dd, ds, sd, ep3, b3, noise, v1, v2, v3,
+           w1, w2, w3, v4, p1d1, p1s1, o1, d1d, s1d, s1s,
            e1, lx, rx, tc, fix, hx1, sx1, hy1, sy1, hc1, sc1, xd1, xs1,
            e2, xl, xh, xlow, xhigh, xd2, xs2, t3d, t3s,
            mine, rows_in, dummy, send, recv, lsem, wsem):
@@ -149,7 +171,7 @@
             greet(*d)
     first_weight = pltpu.make_async_copy(g1, w1, wsem.at[0])
     first_weight.start()
-    more = list(zip((g2, g3, g4, g5, g6), (w2, w3, v1, v2, v3)))
+    more = list(zip((g2, g3, g4, g5, g6, g7), (w2, w3, v1, v2, v3, v4)))
     for src, dst in more:
         pltpu.make_async_copy(src, dst, wsem.at[1]).start()
 
@@ -388,12 +410,9 @@
     noise[...] = jnp.broadcast_to(level, (PAD, LANES))
     far1, mid1, near1 = limits(level, 1)
 
-    def put_into(dst, h):
+    def put_into(dst):
         def put(n, rows):
-            if h is None:
-                dst[n] = rows
-            else:
-                dst[n, h] = rows
+            dst[n] = rows
         return put
 
     def bands1(det, smo, h, limit_d, limit_s):
@@ -402,9 +421,17 @@
             return d, shrink(smo[n, h], limit_s) + d
         return one_x
 
-    for h in range(2):
-        inverse1(hx, bands1(d1d, s1d, h, far1, mid1), put_into(p1d, h))
-    inverse1(hx, bands1(d1s, s1s, 1, mid1, near1), put_into(p1s1, None))
+    inverse1(hx, bands1(d1d, s1d, 1, far1, mid1), put_into(p1d1))
+    inverse1(hx, bands1(d1s, s1s, 1, mid1, near1), put_into(p1s1))
+    inverse1(hx, bands1(d1d, s1d, 0, far1, mid1), put_into(p1d0))
+    layers = 4
+    for n in range(layers):
+        inverse1_y(hy, p1d1, p1s1, n, o1)
+    for lo in range(0, cx, layers):
+        for n in range(lo + layers, min(lo + 2 * layers, cx)):
+            inverse1_y(hy, p1d1, p1s1, n, o1)
+        rows = o1[lo : lo + layers].reshape(layers * cy, LANES)
+        known1[lo : lo + layers] = times_half(rows, v4).reshape(layers, cy, cz)
 
     land(recv.at[3], round2)
     every = slice(0, hy + 2 * PAD)
@@ -456,7 +483,7 @@
     land(send.at[0], sent[0])
 
 
-def finish(shape, d1s, p1d, p1s1, dd, ds, sd, ep3, b3, total, v1, v2, v3, out,
+def finish(shape, d1s, p1d0, known1, dd, ds, sd, ep3, b3, total, v1, v2, v3, out,
            ss, r2, r1, s0, p1s0, o1, ob, osem):
     cx, cy, cz = shape
     hx, hy, qx, qy = cx // 2, cy // 2, cx // 4, cy // 4
@@ -520,28 +547,16 @@
 
     inverse1(hx, low_x, put_low)
 
-    def inv1_y(n):
-        for h in range(2):
-            y_d = p1d[n, h, 0:hy]
-            y_n = p1d[n, h, 1 : hy + 1]
-            p1s = p1s1 if h else p1s0
-            s = p1s[n, PAD : PAD + hy]
-            s_b = p1s[n, PAD - 1 : PAD - 1 + hy]
-            even, odd = undo(y_d, s + y_n, s_b + y_d)
-            o1[n, h, pl.ds(0, hy, stride=2), :] = even
-            o1[n, h, pl.ds(1, hy, stride=2), :] = odd
-
     layers = 4
     outs = []
     for n in range(layers):
-        inv1_y(n)
+        inverse1_y(hy, p1d0, p1s0, n, o1)
     for i in range(cx // layers):
         for n in range((i + 1) * layers, min((i + 2) * layers, cx)):
-            inv1_y(n)
+            inverse1_y(hy, p1d0, p1s0, n, o1)
         xs = slice(i * layers, (i + 1) * layers)
-        rows = jnp.concatenate(
-            [o1[xs, h].reshape(layers * cy, LANES) for h in range(2)], axis=1)
-        ob[xs] = times(rows, v1).reshape(layers, cy, cz)
+        rows = o1[xs].reshape(layers * cy, LANES)
+        ob[xs] = known1[xs] + times_half(rows, v1).reshape(layers, cy, cz)
         c = pltpu.make_async_copy(ob.at[xs], out.at[xs], osem.at[i])
         c.start()
         outs.append(c)
@@ -557,22 +572,23 @@
     count = cx * nx * cy * ny * cz // 8
     weights = [
         halves(forward_matrix(cz), cz), folded(forward_matrix(cz // 2)),
-        folded(forward_matrix(cz // 4)), halves(inverse_matrix(cz), cz),
+        folded(forward_matrix(cz // 4)), half_product(inverse_matrix(cz), 0),
         folded(inverse_matrix(cz // 2)), folded(inverse_matrix(cz // 4)),
+        half_product(inverse_matrix(cz), 1),
     ]
     vmem = lambda *s: pltpu.VMEM(s, f32)
     ey, ey2, ey3 = cy + 2 * PAD, hy + 2 * PAD, qy + 2 * PAD
     wide = lambda *s: pltpu.VMEM(s, jnp.bfloat16)
     pair = (2 * LANES, 2 * LANES)
     made = (
-        vmem(hx + 1, 2, hy + PAD, LANES), vmem(cx, 2, hy + PAD, LANES),
-        vmem(cx, hy + PAD, LANES), *[vmem(qx + 2, ey3, LANES) for _ in range(3)],
+        vmem(hx + 1, 2, hy + PAD, LANES), vmem(cx, hy + PAD, LANES), vmem(cx, cy, cz), *[vmem(qx + 2, ey3, LANES) for _ in range(3)],
         vmem(qx + 4, ey3, LANES), vmem(4, n3, h3, LANES), vmem(PAD, LANES),
-        wide(2, cz, cz), wide(*pair), wide(*pair),
+        wide(3 * LANES, cz), wide(*pair), wide(*pair),
     )
     rows = 4 * cy + 4 * cx + 10 + 6 * (hy + 2 * PAD) + 2 * hx * PAD + nx * ny
     scratch = [
-        wide(2, cz, cz), wide(*pair), wide(*pair),
+        wide(2, cz, cz), wide(*pair), wide(*pair), wide(3 * LANES, cz),
+        vmem(cx, hy + PAD, LANES), vmem(cx, hy + PAD, LANES), vmem(cx, cy, LANES),
         *[vmem(hx + 1, 2, hy + PAD, LANES) for _ in range(3)],
         vmem(cx, 2, ey, LANES), vmem(2, 2, hy, LANES), vmem(2, 2, hy, LANES),
         vmem(2, 1, LANES), vmem(2, ey2, LANES),
@@ -592,7 +608,7 @@
     passed = pl.pallas_call(
         functools.partial(kernel, (cx, cy, cz), count, nx, ny),
         out_shape=made,
-        in_specs=[pl.BlockSpec(memory_space=pltpu.HBM)] * 7,
+        in_specs=[pl.BlockSpec(memory_space=pltpu.HBM)] * 8,
         out_specs=(near,) * len(made),
         scratch_shapes=scratch,
         compiler_params=pltpu.CompilerParams(
@@ -606,7 +622,7 @@
         scratch_shapes=[
             vmem(qx + 2, ey3, LANES), vmem(qx + 2, ey3, LANES), vmem(hx + 2, 2 * ey3, LANES),
             vmem(hx + 1, hy + PAD, LANES),
-            vmem(cx, hy + PAD, LANES), vmem(cx, 2, cy, LANES), vmem(cx, cy, cz), pltpu.SemaphoreType.DMA((cx // 4,)),
+            vmem(cx, hy + PAD, LANES), vmem(cx, cy, LANES), vmem(cx, cy, cz), pltpu.SemaphoreType.DMA((cx // 4,)),
         ],
         compiler_params=pltpu.CompilerParams(vmem_limit_bytes=24 * 1024 * 1024),
     )(*passed)

time: 18.6 us -> 18.3 us (0.984)
  Pallas kernels: 18.4 us -> 18.2 us
    pallas_call x1, Pallas kernels: 2.8 us -> 2.55 us  [on_device(): pl.pallas_call(functools.partial(finish, (cx, cy, cz)), out_shape=jax.Sha...]
where the time goes in v7:
time: 18.3 us; the launch traced here: 18.2 us
  Pallas kernels  18.2 us (99%)
    pallas_call x1, Pallas kernels, on_device(): pl.pallas_call(functools.partial(kernel, (cx, cy, cz), count, nx, ny), ou...  15.6 us
    pallas_call x1, Pallas kernels, on_device(): pl.pallas_call(functools.partial(finish, (cx, cy, cz)), out_shape=jax.Sha...  2.55 us

profile of v7, /device:TPU:0, one launch (start us, length us, event | category | flops | bytes accessed | tf_op | source)
XLA Modules:
  0.0 18.2 jit_solution(16695797572959473021)
XLA Ops:
  0.0 15.6 %shard_map.82 = (f32[17,2,40,128]{3,2,1,0:T(8,128)S(1)}, f32[32,40,128]{2,1,0:T(8,128)S(1)}, f32[32,64,256]{2,1,0:T(8,128)S(1)}, f32[10,32,128]{2,1,0:T(8,128)S(...) custom-call(f32[32,64,256]{2,1,0:T(8,128)} %vol.1, ...), custom_call_target="tpu_custom_call" | custom-call | tf_op jit(solution)/shard_map/pallas_call | solution.py:608
  15.6 2.6 %shard_map.83 = f32[32,64,256]{2,1,0:T(8,128)} custom-call(f32[17,2,40,128]{3,2,1,0:T(8,128)S(1)} %get-tuple-element.17.d1s, f32[32,40,128]{2,1,0:T(8,128)S(1)} %get-tuple-element.18.p1d0, f32[32,64,256]{2,1,0:T(8,128)S(1)} %get-tuple-element.19.known1, f32[10,32,128]{2,1,0:T(8,128)S(1)} %get-tuple-element.20.dd, f32[10,32,128]{2,1,0:T(8,128)S(1)} %get-tuple-element.21.ds, ...), custom_call_target="tpu_custom_call" | custom-call | tf_op jit(solution)/shard_map/pallas_call | solution.py:617

commit v8 on v7

--- a/solution.py
+++ b/solution.py
@@ -114,7 +114,7 @@
         HIGH * HIGH * math.sqrt(math.pi / 2.0) / count_all)
 
 
-def inverse1(hx, one_x, put):
+def inverse1(hx, one_x, put, unroll=4):
     def step(n, carry):
         d, before = carry
         after, one = one_x(n + 1)
@@ -123,7 +123,7 @@
         put(2 * n + 1, odd)
         return after, one
 
-    lax.fori_loop(0, hx, step, one_x(0), unroll=4)
+    lax.fori_loop(0, hx, step, one_x(0), unroll=unroll)
 
 
 def inverse1_y(hy, det, smo, n, dst):
@@ -423,13 +423,18 @@
 
     inverse1(hx, bands1(d1d, s1d, 1, far1, mid1), put_into(p1d1))
     inverse1(hx, bands1(d1s, s1s, 1, mid1, near1), put_into(p1s1))
-    inverse1(hx, bands1(d1d, s1d, 0, far1, mid1), put_into(p1d0))
     layers = 4
+    detail_x = bands1(d1d, s1d, 0, far1, mid1)
+    carry = detail_x(0)
     for n in range(layers):
         inverse1_y(hy, p1d1, p1s1, n, o1)
     for lo in range(0, cx, layers):
         for n in range(lo + layers, min(lo + 2 * layers, cx)):
             inverse1_y(hy, p1d1, p1s1, n, o1)
+        for n in range(lo // 2, (lo + layers) // 2):
+            d, before = carry
+            carry = detail_x(n + 1)
+            p1d0[2 * n], p1d0[2 * n + 1] = undo(d, carry[1], before)
         rows = o1[lo : lo + layers].reshape(layers * cy, LANES)
         known1[lo : lo + layers] = times_half(rows, v4).reshape(layers, cy, cz)
 
@@ -477,8 +482,8 @@
     bands = []
     for src in (t3d, t3s):
         bands += forward_rows(src[:, pl.ds(0, h3, stride=2), :], src[:, pl.ds(1, h3, stride=2), :])
-    for i, band in enumerate(bands):
-        b3[i] = times_folded(band.reshape(n3 * h3, LANES), w3).reshape(n3, h3, LANES)
+    rows = jnp.concatenate([band.reshape(n3 * h3, LANES) for band in bands], axis=0)
+    b3[...] = times_folded(rows, w3).reshape(len(bands), n3, h3, LANES)
 
     land(send.at[0], sent[0])
 
@@ -532,10 +537,15 @@
             r1[2 * n + i, pl.ds(1, yrows, stride=2), :] = odd
         return after
 
-    lax.fori_loop(0, qx + 1, inv2, one_x(0), unroll=True)
-    x1, y1 = hx + 2, hy + PAD
-    back = times_folded(r1[:, PAD : PAD + y1].reshape(x1 * y1, LANES), v2).reshape(x1, y1, LANES)
-    s0[...] = back[1:]
+    y1, group = hy + PAD, 3
+    carry = one_x(0)
+    for n in range(qx + 1):
+        carry = inv2(n, carry)
+        if (n + 1) % group == 0 or n == qx:
+            lo, hi = 2 * (n // group * group), 2 * n + 2
+            back = times_folded(r1[lo:hi, PAD : PAD + y1].reshape((hi - lo) * y1, LANES), v2)
+            back = back.reshape(hi - lo, y1, LANES)
+            s0[max(lo - 1, 0) : hi - 1] = back[1:] if lo == 0 else back
     _, mid1, _ = limits(noise, 1)
 
     def low_x(n):
@@ -545,10 +555,9 @@
     def put_low(n, rows):
         p1s0[n] = rows
 
-    inverse1(hx, low_x, put_low)
+    inverse1(hx, low_x, put_low, True)
 
     layers = 4
-    outs = []
     for n in range(layers):
         inverse1_y(hy, p1d0, p1s0, n, o1)
     for i in range(cx // layers):
@@ -557,11 +566,9 @@
         xs = slice(i * layers, (i + 1) * layers)
         rows = o1[xs].reshape(layers * cy, LANES)
         ob[xs] = known1[xs] + times_half(rows, v1).reshape(layers, cy, cz)
-        c = pltpu.make_async_copy(ob.at[xs], out.at[xs], osem.at[i])
-        c.start()
-        outs.append(c)
-    for c in outs:
-        c.wait()
+        for n in range(i * layers, (i + 1) * layers):
+            pltpu.make_async_copy(ob.at[n], out.at[n], osem.at[0]).start()
+    pltpu.make_async_copy(ob, out, osem.at[0]).wait()
 
 
 def on_device(nx, ny, volume):
@@ -622,7 +629,7 @@
         scratch_shapes=[
             vmem(qx + 2, ey3, LANES), vmem(qx + 2, ey3, LANES), vmem(hx + 2, 2 * ey3, LANES),
             vmem(hx + 1, hy + PAD, LANES),
-            vmem(cx, hy + PAD, LANES), vmem(cx, cy, LANES), vmem(cx, cy, cz), pltpu.SemaphoreType.DMA((cx // 4,)),
+            vmem(cx, hy + PAD, LANES), vmem(cx, cy, LANES), vmem(cx, cy, cz), pltpu.SemaphoreType.DMA((1,)),
         ],
         compiler_params=pltpu.CompilerParams(vmem_limit_bytes=24 * 1024 * 1024),
     )(*passed)

time: 18.3 us -> 18.1 us (0.989)
  Pallas kernels: 18.2 us -> 18 us
    pallas_call x1, Pallas kernels: 2.55 us -> 2.34 us  [on_device(): pl.pallas_call(functools.partial(finish, (cx, cy, cz)), out_shape=jax.Sha...]
where the time goes in v8:
time: 18.1 us; the launch traced here: 18 us
  Pallas kernels  18 us (99%)
    pallas_call x1, Pallas kernels, on_device(): pl.pallas_call(functools.partial(kernel, (cx, cy, cz), count, nx, ny), ou...  15.6 us
    pallas_call x1, Pallas kernels, on_device(): pl.pallas_call(functools.partial(finish, (cx, cy, cz)), out_shape=jax.Sha...  2.34 us

profile of v8, /device:TPU:0, one launch (start us, length us, event | category | flops | bytes accessed | tf_op | source)
XLA Modules:
  0.0 18.0 jit_solution(14833536981684896342)
XLA Ops:
  0.0 15.6 %shard_map.82 = (f32[17,2,40,128]{3,2,1,0:T(8,128)S(1)}, f32[32,40,128]{2,1,0:T(8,128)S(1)}, f32[32,64,256]{2,1,0:T(8,128)S(1)}, f32[10,32,128]{2,1,0:T(8,128)S(...) custom-call(f32[32,64,256]{2,1,0:T(8,128)} %vol.1, ...), custom_call_target="tpu_custom_call" | custom-call | tf_op jit(solution)/shard_map/pallas_call | solution.py:615
  15.6 2.3 %shard_map.83 = f32[32,64,256]{2,1,0:T(8,128)} custom-call(f32[17,2,40,128]{3,2,1,0:T(8,128)S(1)} %get-tuple-element.17.d1s, f32[32,40,128]{2,1,0:T(8,128)S(1)} %get-tuple-element.18.p1d0, f32[32,64,256]{2,1,0:T(8,128)S(1)} %get-tuple-element.19.known1, f32[10,32,128]{2,1,0:T(8,128)S(1)} %get-tuple-element.20.dd, f32[10,32,128]{2,1,0:T(8,128)S(1)} %get-tuple-element.21.ds, ...), custom_call_target="tpu_custom_call" | custom-call | tf_op jit(solution)/shard_map/pallas_call | solution.py:624

commit v9 on v8

--- a/solution.py
+++ b/solution.py
@@ -423,7 +423,7 @@
 
     inverse1(hx, bands1(d1d, s1d, 1, far1, mid1), put_into(p1d1))
     inverse1(hx, bands1(d1s, s1s, 1, mid1, near1), put_into(p1s1))
-    layers = 4
+    layers = 2
     detail_x = bands1(d1d, s1d, 0, far1, mid1)
     carry = detail_x(0)
     for n in range(layers):
@@ -557,7 +557,7 @@
 
     inverse1(hx, low_x, put_low, True)
 
-    layers = 4
+    layers = 2
     for n in range(layers):
         inverse1_y(hy, p1d0, p1s0, n, o1)
     for i in range(cx // layers):

time: 18.1 us -> 18 us (level)
  Pallas kernels: 18 us -> 17.8 us
where the time goes in v9:
time: 18 us; the launch traced here: 17.9 us
  Pallas kernels  17.8 us (99%)
    pallas_call x1, Pallas kernels, on_device(): pl.pallas_call(functools.partial(kernel, (cx, cy, cz), count, nx, ny), ou...  15.6 us
    pallas_call x1, Pallas kernels, on_device(): pl.pallas_call(functools.partial(finish, (cx, cy, cz)), out_shape=jax.Sha...  2.22 us

profile of v9, /device:TPU:0, one launch (start us, length us, event | category | flops | bytes accessed | tf_op | source)
XLA Modules:
  0.0 17.9 jit_solution(15076907943766996355)
XLA Ops:
  0.0 15.6 %shard_map.82 = (f32[17,2,40,128]{3,2,1,0:T(8,128)S(1)}, f32[32,40,128]{2,1,0:T(8,128)S(1)}, f32[32,64,256]{2,1,0:T(8,128)S(1)}, f32[10,32,128]{2,1,0:T(8,128)S(...) custom-call(f32[32,64,256]{2,1,0:T(8,128)} %vol.1, ...), custom_call_target="tpu_custom_call" | custom-call | tf_op jit(solution)/shard_map/pallas_call | solution.py:615
  15.6 2.2 %shard_map.83 = f32[32,64,256]{2,1,0:T(8,128)} custom-call(f32[17,2,40,128]{3,2,1,0:T(8,128)S(1)} %get-tuple-element.17.d1s, f32[32,40,128]{2,1,0:T(8,128)S(1)} %get-tuple-element.18.p1d0, f32[32,64,256]{2,1,0:T(8,128)S(1)} %get-tuple-element.19.known1, f32[10,32,128]{2,1,0:T(8,128)S(1)} %get-tuple-element.20.dd, f32[10,32,128]{2,1,0:T(8,128)S(1)} %get-tuple-element.21.ds, ...), custom_call_target="tpu_custom_call" | custom-call | tf_op jit(solution)/shard_map/pallas_call | solution.py:624

commit v10 on v9

--- a/solution.py
+++ b/solution.py
@@ -149,6 +149,7 @@
 
     near = [(dx, dy) for dx in (-1, 0, 1) for dy in (-1, 0, 1) if dx or dy]
     peers = [(dx, dy) for dx in range(nx) for dy in range(ny) if dx or dy]
+    peers.sort(key=lambda d: (d[0] % 2 == 0, d[0], min(d[1], ny - d[1])))
     taken = {(dx % nx, dy % ny) for dx, dy in near}
     barrier = pltpu.get_barrier_semaphore()
 

time: 18 us -> 17.9 us (level)
  no operation moved by 1% of the time
where the time goes in v10:
time: 17.9 us; the launch traced here: 17.8 us
  Pallas kernels  17.8 us (99%)
    pallas_call x1, Pallas kernels, on_device(): pl.pallas_call(functools.partial(kernel, (cx, cy, cz), count, nx, ny), ou...  15.6 us
    pallas_call x1, Pallas kernels, on_device(): pl.pallas_call(functools.partial(finish, (cx, cy, cz)), out_shape=jax.Sha...  2.22 us

profile of v10, /device:TPU:0, one launch (start us, length us, event | category | flops | bytes accessed | tf_op | source)
XLA Modules:
  0.0 17.8 jit_solution(407200924530463122)
XLA Ops:
  0.0 15.6 %shard_map.82 = (f32[17,2,40,128]{3,2,1,0:T(8,128)S(1)}, f32[32,40,128]{2,1,0:T(8,128)S(1)}, f32[32,64,256]{2,1,0:T(8,128)S(1)}, f32[10,32,128]{2,1,0:T(8,128)S(...) custom-call(f32[32,64,256]{2,1,0:T(8,128)} %vol.1, ...), custom_call_target="tpu_custom_call" | custom-call | tf_op jit(solution)/shard_map/pallas_call | solution.py:616
  15.6 2.2 %shard_map.83 = f32[32,64,256]{2,1,0:T(8,128)} custom-call(f32[17,2,40,128]{3,2,1,0:T(8,128)S(1)} %get-tuple-element.17.d1s, f32[32,40,128]{2,1,0:T(8,128)S(1)} %get-tuple-element.18.p1d0, f32[32,64,256]{2,1,0:T(8,128)S(1)} %get-tuple-element.19.known1, f32[10,32,128]{2,1,0:T(8,128)S(1)} %get-tuple-element.20.dd, f32[10,32,128]{2,1,0:T(8,128)S(1)} %get-tuple-element.21.ds, ...), custom_call_target="tpu_custom_call" | custom-call | tf_op jit(solution)/shard_map/pallas_call | solution.py:625

commit v11 on v10

--- a/solution.py
+++ b/solution.py
@@ -422,8 +422,15 @@
             return d, shrink(smo[n, h], limit_s) + d
         return one_x
 
-    inverse1(hx, bands1(d1d, s1d, 1, far1, mid1), put_into(p1d1))
-    inverse1(hx, bands1(d1s, s1s, 1, mid1, near1), put_into(p1s1))
+    high_d, high_s = bands1(d1d, s1d, 1, far1, mid1), bands1(d1s, s1s, 1, mid1, near1)
+
+    def high_x(n, carry):
+        new = high_d(n + 1) + high_s(n + 1)
+        p1d1[2 * n], p1d1[2 * n + 1] = undo(carry[0], new[1], carry[1])
+        p1s1[2 * n], p1s1[2 * n + 1] = undo(carry[2], new[3], carry[3])
+        return new
+
+    lax.fori_loop(0, hx, high_x, high_d(0) + high_s(0), unroll=4)
     layers = 2
     detail_x = bands1(d1d, s1d, 0, far1, mid1)
     carry = detail_x(0)

time: 17.9 us -> 17.9 us (level)
  no operation moved by 1% of the time
where the time goes in v11:
time: 17.9 us; the launch traced here: 17.8 us
  Pallas kernels  17.7 us (99%)
    pallas_call x1, Pallas kernels, on_device(): pl.pallas_call(functools.partial(kernel, (cx, cy, cz), count, nx, ny), ou...  15.5 us
    pallas_call x1, Pallas kernels, on_device(): pl.pallas_call(functools.partial(finish, (cx, cy, cz)), out_shape=jax.Sha...  2.22 us

profile of v11, /device:TPU:0, one launch (start us, length us, event | category | flops | bytes accessed | tf_op | source)
XLA Modules:
  0.0 17.8 jit_solution(15256030834122837323)
XLA Ops:
  0.0 15.5 %shard_map.82 = (f32[17,2,40,128]{3,2,1,0:T(8,128)S(1)}, f32[32,40,128]{2,1,0:T(8,128)S(1)}, f32[32,64,256]{2,1,0:T(8,128)S(1)}, f32[10,32,128]{2,1,0:T(8,128)S(...) custom-call(f32[32,64,256]{2,1,0:T(8,128)} %vol.1, ...), custom_call_target="tpu_custom_call" | custom-call | tf_op jit(solution)/shard_map/pallas_call | solution.py:623
  15.5 2.2 %shard_map.83 = f32[32,64,256]{2,1,0:T(8,128)} custom-call(f32[17,2,40,128]{3,2,1,0:T(8,128)S(1)} %get-tuple-element.17.d1s, f32[32,40,128]{2,1,0:T(8,128)S(1)} %get-tuple-element.18.p1d0, f32[32,64,256]{2,1,0:T(8,128)S(1)} %get-tuple-element.19.known1, f32[10,32,128]{2,1,0:T(8,128)S(1)} %get-tuple-element.20.dd, f32[10,32,128]{2,1,0:T(8,128)S(1)} %get-tuple-element.21.ds, ...), custom_call_target="tpu_custom_call" | custom-call | tf_op jit(solution)/shard_map/pallas_call | solution.py:632
